TPU v7x, 32 devices: a 4x2x2 block of a 4x4x8 slice. The times are simulated.
32 devices in a mesh: dp: 4 (over y, z), stage: 8 (over x, core).
Axes of the slice: x: 4, y: 2, z: 2, core: 2. Of those that a mesh axis runs over, the one named last changes fastest.
The devices are a block of a 4x4x8 slice.
Arguments:
- tokens: int32 [64, 64], P('dp'), parts along dimension 0
- labels: int32 [64, 64], P('dp'), parts along dimension 0
- emb_table: bfloat16 [30592, 128], replicated
- w_up: bfloat16 [8, 128, 512], P('stage')
- w_down: bfloat16 [8, 512, 128], P('stage')
Outputs:
- output 1: float32 [4], P('dp'), parts along dimension 0
- output 2: float32 [32, 128, 512], P(('dp', 'stage')), parts along dimension 0
- output 3: float32 [32, 512, 128], P(('dp', 'stage')), parts along dimension 0
- output 4: float32 [122368, 128], P('dp'), parts along dimension 0
There are 4 independent parts. A program takes and returns all parts, laid end to end along the dimension named above; an argument that names none is the same for every part.
All inputs are finite; a program needn't handle non-finite values.
Results may differ from a plain program's by a relative error of at most 0.02.
Values are sent between devices in bfloat16 or wider.
A program may use at most 768 MiB of HBM per device.

v0:
```python
import jax
import jax.numpy as jnp
from jax import lax
from jax.sharding import PartitionSpec as P


def rms_normalize(x_act):
    x_wide = x_act.astype(jnp.float32)
    inv_rms = lax.rsqrt(jnp.mean(x_wide * x_wide, axis=-1, keepdims=True) + 1e-6)
    return (x_wide * inv_rms).astype(jnp.bfloat16)


def block_forward(x_act, w_up, w_down):
    pre_act = jnp.dot(x_act, w_up, preferred_element_type=jnp.float32).astype(jnp.bfloat16)
    hidden = jax.nn.gelu(pre_act.astype(jnp.float32)).astype(jnp.bfloat16)
    branch = jnp.dot(hidden, w_down, preferred_element_type=jnp.float32)
    return (x_act.astype(jnp.float32) + branch).astype(jnp.bfloat16), pre_act, hidden


def block_backward(x_act, pre_act, hidden, grad_out, w_up, w_down):
    grad_down = jnp.einsum("tf,td->fd", hidden, grad_out, preferred_element_type=jnp.float32)
    grad_hidden = jnp.einsum("td,fd->tf", grad_out, w_down, preferred_element_type=jnp.float32).astype(jnp.bfloat16)
    gelu_vjp = jax.vjp(jax.nn.gelu, pre_act.astype(jnp.float32))[1]
    grad_pre = gelu_vjp(grad_hidden.astype(jnp.float32))[0].astype(jnp.bfloat16)
    grad_up = jnp.einsum("td,tf->df", x_act, grad_pre, preferred_element_type=jnp.float32)
    back_flow = jnp.einsum("tf,df->td", grad_pre, w_up, preferred_element_type=jnp.float32)
    grad_in = (grad_out.astype(jnp.float32) + back_flow).astype(jnp.bfloat16)
    return grad_in, grad_up, grad_down


def head_step(x_act, lab_row, emb_table, grad_emb, inv_count):
    logit_scale = emb_table.shape[1] ** -0.5
    normed, norm_vjp = jax.vjp(rms_normalize, x_act)
    logits = (jnp.einsum("td,vd->tv", normed, emb_table, preferred_element_type=jnp.float32) * logit_scale).astype(jnp.bfloat16)
    logit_f = logits.astype(jnp.float32)
    row_max = jnp.max(logit_f, axis=-1, keepdims=True)
    exp_shift = jnp.exp(logit_f - row_max)
    exp_total = jnp.sum(exp_shift, axis=-1, keepdims=True)
    is_label = lax.broadcasted_iota(jnp.int32, logit_f.shape, 1) == lab_row[:, None]
    picked = jnp.sum(jnp.where(is_label, logit_f, 0.0), axis=-1)
    loss_part = jnp.sum(row_max[:, 0] + jnp.log(exp_total[:, 0]) - picked) * inv_count
    grad_logits = ((exp_shift / exp_total - is_label.astype(jnp.float32)) * inv_count).astype(jnp.bfloat16)
    grad_emb = grad_emb + jnp.einsum("tv,td->vd", grad_logits, normed, preferred_element_type=jnp.float32) * logit_scale
    grad_normed = (jnp.einsum("tv,vd->td", grad_logits, emb_table, preferred_element_type=jnp.float32) * logit_scale).astype(jnp.bfloat16)
    return norm_vjp(grad_normed)[0], grad_emb, loss_part


def solution(mesh):
    n_stage = mesh.shape["stage"]
    fwd_perm = [(stage_id, stage_id + 1) for stage_id in range(n_stage - 1)]
    bwd_perm = [(stage_id + 1, stage_id) for stage_id in range(n_stage - 1)]

    def device_fn(tokens, labels, emb_table, w_up, w_down):
        n_micro, seq_len = tokens.shape
        vocab_rows, model_dim = emb_table.shape
        w_up = w_up[0]
        w_down = w_down[0]
        ffn_dim = w_up.shape[1]
        stage_idx = lax.axis_index("stage")
        is_first = stage_idx == 0
        is_last = stage_idx == n_stage - 1
        n_slots = min(n_micro, 2 * n_stage - 1)
        n_ticks = n_micro + 2 * n_stage - 2
        inv_count = 1.0 / (n_micro * seq_len)

        def tick(tick_idx, loop_state):
            recv_act, recv_grad, stash_x, stash_pre, stash_hid, acc_up, acc_down, grad_emb, loss_acc = loop_state
            micro_f = tick_idx - stage_idx
            fwd_ok = (micro_f >= 0) & (micro_f < n_micro)
            idx_f = jnp.clip(micro_f, 0, n_micro - 1)
            slot_f = idx_f % n_slots
            micro_b = tick_idx - (2 * n_stage - 2) + stage_idx
            bwd_ok = (micro_b >= 0) & (micro_b < n_micro)
            idx_b = jnp.clip(micro_b, 0, n_micro - 1)
            slot_b = idx_b % n_slots
            tok_f = lax.dynamic_index_in_dim(tokens, idx_f, 0, keepdims=False)
            lab_f = lax.dynamic_index_in_dim(labels, idx_f, 0, keepdims=False)
            x_in = jnp.where(is_first, jnp.take(emb_table, tok_f, axis=0), recv_act)

            def run_fwd(branch_in):
                y_out, pre_act, hidden = block_forward(x_in, w_up, w_down)
                return (y_out, lax.dynamic_update_index_in_dim(branch_in[0], x_in, slot_f, 0), lax.dynamic_update_index_in_dim(branch_in[1], pre_act, slot_f, 0), lax.dynamic_update_index_in_dim(branch_in[2], hidden, slot_f, 0))

            def skip_fwd(branch_in):
                return (jnp.zeros_like(x_in),) + branch_in

            y_out, stash_x, stash_pre, stash_hid = lax.cond(fwd_ok, run_fwd, skip_fwd, (stash_x, stash_pre, stash_hid))

            def run_head(branch_in):
                grad_x, new_emb, loss_part = head_step(y_out, lab_f, emb_table, branch_in[0], inv_count)
                return grad_x, new_emb, branch_in[1] + loss_part

            def skip_head(branch_in):
                return jnp.zeros_like(y_out), branch_in[0], branch_in[1]

            head_grad, grad_emb, loss_acc = lax.cond(is_last & fwd_ok, run_head, skip_head, (grad_emb, loss_acc))
            grad_out = jnp.where(is_last, head_grad, recv_grad)

            def run_bwd(branch_in):
                x_saved = lax.dynamic_index_in_dim(stash_x, slot_b, 0, keepdims=False)
                pre_saved = lax.dynamic_index_in_dim(stash_pre, slot_b, 0, keepdims=False)
                hid_saved = lax.dynamic_index_in_dim(stash_hid, slot_b, 0, keepdims=False)
                grad_in, g_up, g_down = block_backward(x_saved, pre_saved, hid_saved, grad_out, w_up, w_down)
                return grad_in, branch_in[0] + g_up, branch_in[1] + g_down

            def skip_bwd(branch_in):
                return jnp.zeros_like(grad_out), branch_in[0], branch_in[1]

            grad_in, acc_up, acc_down = lax.cond(bwd_ok, run_bwd, skip_bwd, (acc_up, acc_down))
            tok_b = lax.dynamic_index_in_dim(tokens, idx_b, 0, keepdims=False)
            emb_rows = jnp.where(is_first, grad_in, jnp.zeros_like(grad_in)).astype(jnp.float32)
            grad_emb = grad_emb.at[tok_b].add(emb_rows)
            recv_act = lax.ppermute(y_out, "stage", fwd_perm)
            recv_grad = lax.ppermute(grad_in, "stage", bwd_perm)
            return (recv_act, recv_grad, stash_x, stash_pre, stash_hid, acc_up, acc_down, grad_emb, loss_acc)

        zeros_act = jnp.zeros((seq_len, model_dim), jnp.bfloat16)
        init_carry = (zeros_act, zeros_act, jnp.zeros((n_slots, seq_len, model_dim), jnp.bfloat16), jnp.zeros((n_slots, seq_len, ffn_dim), jnp.bfloat16), jnp.zeros((n_slots, seq_len, ffn_dim), jnp.bfloat16), jnp.zeros((model_dim, ffn_dim), jnp.float32), jnp.zeros((ffn_dim, model_dim), jnp.float32), jnp.zeros((vocab_rows, model_dim), jnp.float32), jnp.zeros((), jnp.float32))
        final_state = lax.fori_loop(0, n_ticks, tick, init_carry)
        grad_emb = lax.psum(final_state[7], "stage")
        loss_total = lax.psum(final_state[8], "stage")
        return loss_total.reshape(1), final_state[5][None], final_state[6][None], grad_emb

    return jax.shard_map(device_fn, mesh=mesh, in_specs=(P("dp", None), P("dp", None), P(None, None), P("stage", None, None), P("stage", None, None)), out_specs=(P("dp"), P(("dp", "stage"), None, None), P(("dp", "stage"), None, None), P("dp", None)), check_vma=False)
```

profile of v0, /device:TPU:81, one launch (start us, length us, event | category | flops | bytes accessed | tf_op | source)
XLA Modules:
  0.0 1388.2 jit_solution(16766848092947663985)
XLA Ops:
  13.6 1187.3 %while.31 = (s32[]{:T(128)}, bf16[64,128]{1,0:T(8,128)(2,1)S(1)}, bf16[64,128]{1,0:T(8,128)(2,1)S(1)}, bf16[15,64,128]{2,1,0:T(8,128)(2,1)S(1)}, bf16[15,64,512]...) while((s32[]{:T(128)}, bf16[64,128]{1,0:T(8,128)(2,1)S(1)}, ...), condition=%wide.region_14.15_spmd, body=%wide.region_0.14_spmd.sunk | while | flops 1612613888 | bytes 96764176 | solution.py:119
  27.1 12.1 scatter_custom_fusion.5
  51.7 12.1 scatter_custom_fusion.5
  77.2 12.1 scatter_custom_fusion.5
  103.1 12.1 scatter_custom_fusion.5
  154.9 12.1 scatter_custom_fusion.5
  180.8 12.1 scatter_custom_fusion.5
  206.7 12.1 scatter_custom_fusion.5
  258.6 12.1 scatter_custom_fusion.5
  284.5 12.1 scatter_custom_fusion.5
  303.9 19.3 %collective-permute-start = (bf16[64,128]{1,0:T(8,128)(2,1)}, bf16[64,128]{1,0:T(8,128)(2,1)S(1)}, u32[]{:S(2)}, u32[]{:S(2)}) collective-permute-start(bf16[64,128]{1,0:T(8,128)(2,1)} %get-tuple-element.1044), channel_id=1, source_target_pairs={{0,1},{1,2},{2,3},{3,4},{4,5},{5,6},{6,7},{8,9},{9,10},{10,11},{11... | collective-permute-start | bytes 49160 | tf_op jit(solution)/shard_map/while/body/eval_jaxpr/ppermute | solution.py:113
  348.6 30.6 %collective-permute-start = (bf16[64,128]{1,0:T(8,128)(2,1)}, bf16[64,128]{1,0:T(8,128)(2,1)S(1)}, u32[]{:S(2)}, u32[]{:S(2)}) collective-permute-start(bf16[64,128]{1,0:T(8,128)(2,1)} %get-tuple-element.1044), channel_id=1, source_target_pairs={{0,1},{1,2},{2,3},{3,4},{4,5},{5,6},{6,7},{8,9},{9,10},{10,11},{11... | collective-permute-start | bytes 49160 | tf_op jit(solution)/shard_map/while/body/eval_jaxpr/ppermute | solution.py:113
  381.9 12.1 scatter_custom_fusion.5
  404.5 29.7 %collective-permute-start = (bf16[64,128]{1,0:T(8,128)(2,1)}, bf16[64,128]{1,0:T(8,128)(2,1)S(1)}, u32[]{:S(2)}, u32[]{:S(2)}) collective-permute-start(bf16[64,128]{1,0:T(8,128)(2,1)} %get-tuple-element.1044), channel_id=1, source_target_pairs={{0,1},{1,2},{2,3},{3,4},{4,5},{5,6},{6,7},{8,9},{9,10},{10,11},{11... | collective-permute-start | bytes 49160 | tf_op jit(solution)/shard_map/while/body/eval_jaxpr/ppermute | solution.py:113
  459.5 29.7 %collective-permute-start = (bf16[64,128]{1,0:T(8,128)(2,1)}, bf16[64,128]{1,0:T(8,128)(2,1)S(1)}, u32[]{:S(2)}, u32[]{:S(2)}) collective-permute-start(bf16[64,128]{1,0:T(8,128)(2,1)} %get-tuple-element.1044), channel_id=1, source_target_pairs={{0,1},{1,2},{2,3},{3,4},{4,5},{5,6},{6,7},{8,9},{9,10},{10,11},{11... | collective-permute-start | bytes 49160 | tf_op jit(solution)/shard_map/while/body/eval_jaxpr/ppermute | solution.py:113
  514.6 29.7 %collective-permute-start = (bf16[64,128]{1,0:T(8,128)(2,1)}, bf16[64,128]{1,0:T(8,128)(2,1)S(1)}, u32[]{:S(2)}, u32[]{:S(2)}) collective-permute-start(bf16[64,128]{1,0:T(8,128)(2,1)} %get-tuple-element.1044), channel_id=1, source_target_pairs={{0,1},{1,2},{2,3},{3,4},{4,5},{5,6},{6,7},{8,9},{9,10},{10,11},{11... | collective-permute-start | bytes 49160 | tf_op jit(solution)/shard_map/while/body/eval_jaxpr/ppermute | solution.py:113
  569.6 29.7 %collective-permute-start = (bf16[64,128]{1,0:T(8,128)(2,1)}, bf16[64,128]{1,0:T(8,128)(2,1)S(1)}, u32[]{:S(2)}, u32[]{:S(2)}) collective-permute-start(bf16[64,128]{1,0:T(8,128)(2,1)} %get-tuple-element.1044), channel_id=1, source_target_pairs={{0,1},{1,2},{2,3},{3,4},{4,5},{5,6},{6,7},{8,9},{9,10},{10,11},{11... | collective-permute-start | bytes 49160 | tf_op jit(solution)/shard_map/while/body/eval_jaxpr/ppermute | solution.py:113
  618.0 36.4 %collective-permute-start = (bf16[64,128]{1,0:T(8,128)(2,1)}, bf16[64,128]{1,0:T(8,128)(2,1)S(1)}, u32[]{:S(2)}, u32[]{:S(2)}) collective-permute-start(bf16[64,128]{1,0:T(8,128)(2,1)} %get-tuple-element.1044), channel_id=1, source_target_pairs={{0,1},{1,2},{2,3},{3,4},{4,5},{5,6},{6,7},{8,9},{9,10},{10,11},{11... | collective-permute-start | bytes 49160 | tf_op jit(solution)/shard_map/while/body/eval_jaxpr/ppermute | solution.py:113
  673.0 29.7 %collective-permute-start = (bf16[64,128]{1,0:T(8,128)(2,1)}, bf16[64,128]{1,0:T(8,128)(2,1)S(1)}, u32[]{:S(2)}, u32[]{:S(2)}) collective-permute-start(bf16[64,128]{1,0:T(8,128)(2,1)} %get-tuple-element.1044), channel_id=1, source_target_pairs={{0,1},{1,2},{2,3},{3,4},{4,5},{5,6},{6,7},{8,9},{9,10},{10,11},{11... | collective-permute-start | bytes 49160 | tf_op jit(solution)/shard_map/while/body/eval_jaxpr/ppermute | solution.py:113
  728.1 29.7 %collective-permute-start = (bf16[64,128]{1,0:T(8,128)(2,1)}, bf16[64,128]{1,0:T(8,128)(2,1)S(1)}, u32[]{:S(2)}, u32[]{:S(2)}) collective-permute-start(bf16[64,128]{1,0:T(8,128)(2,1)} %get-tuple-element.1044), channel_id=1, source_target_pairs={{0,1},{1,2},{2,3},{3,4},{4,5},{5,6},{6,7},{8,9},{9,10},{10,11},{11... | collective-permute-start | bytes 49160 | tf_op jit(solution)/shard_map/while/body/eval_jaxpr/ppermute | solution.py:113
  776.4 36.4 %collective-permute-start = (bf16[64,128]{1,0:T(8,128)(2,1)}, bf16[64,128]{1,0:T(8,128)(2,1)S(1)}, u32[]{:S(2)}, u32[]{:S(2)}) collective-permute-start(bf16[64,128]{1,0:T(8,128)(2,1)} %get-tuple-element.1044), channel_id=1, source_target_pairs={{0,1},{1,2},{2,3},{3,4},{4,5},{5,6},{6,7},{8,9},{9,10},{10,11},{11... | collective-permute-start | bytes 49160 | tf_op jit(solution)/shard_map/while/body/eval_jaxpr/ppermute | solution.py:113
  831.4 29.7 %collective-permute-start = (bf16[64,128]{1,0:T(8,128)(2,1)}, bf16[64,128]{1,0:T(8,128)(2,1)S(1)}, u32[]{:S(2)}, u32[]{:S(2)}) collective-permute-start(bf16[64,128]{1,0:T(8,128)(2,1)} %get-tuple-element.1044), channel_id=1, source_target_pairs={{0,1},{1,2},{2,3},{3,4},{4,5},{5,6},{6,7},{8,9},{9,10},{10,11},{11... | collective-permute-start | bytes 49160 | tf_op jit(solution)/shard_map/while/body/eval_jaxpr/ppermute | solution.py:113
  886.5 29.7 %collective-permute-start = (bf16[64,128]{1,0:T(8,128)(2,1)}, bf16[64,128]{1,0:T(8,128)(2,1)S(1)}, u32[]{:S(2)}, u32[]{:S(2)}) collective-permute-start(bf16[64,128]{1,0:T(8,128)(2,1)} %get-tuple-element.1044), channel_id=1, source_target_pairs={{0,1},{1,2},{2,3},{3,4},{4,5},{5,6},{6,7},{8,9},{9,10},{10,11},{11... | collective-permute-start | bytes 49160 | tf_op jit(solution)/shard_map/while/body/eval_jaxpr/ppermute | solution.py:113
  934.8 36.4 %collective-permute-start = (bf16[64,128]{1,0:T(8,128)(2,1)}, bf16[64,128]{1,0:T(8,128)(2,1)S(1)}, u32[]{:S(2)}, u32[]{:S(2)}) collective-permute-start(bf16[64,128]{1,0:T(8,128)(2,1)} %get-tuple-element.1044), channel_id=1, source_target_pairs={{0,1},{1,2},{2,3},{3,4},{4,5},{5,6},{6,7},{8,9},{9,10},{10,11},{11... | collective-permute-start | bytes 49160 | tf_op jit(solution)/shard_map/while/body/eval_jaxpr/ppermute | solution.py:113
  989.8 29.7 %collective-permute-start = (bf16[64,128]{1,0:T(8,128)(2,1)}, bf16[64,128]{1,0:T(8,128)(2,1)S(1)}, u32[]{:S(2)}, u32[]{:S(2)}) collective-permute-start(bf16[64,128]{1,0:T(8,128)(2,1)} %get-tuple-element.1044), channel_id=1, source_target_pairs={{0,1},{1,2},{2,3},{3,4},{4,5},{5,6},{6,7},{8,9},{9,10},{10,11},{11... | collective-permute-start | bytes 49160 | tf_op jit(solution)/shard_map/while/body/eval_jaxpr/ppermute | solution.py:113
  1044.9 29.7 %collective-permute-start = (bf16[64,128]{1,0:T(8,128)(2,1)}, bf16[64,128]{1,0:T(8,128)(2,1)S(1)}, u32[]{:S(2)}, u32[]{:S(2)}) collective-permute-start(bf16[64,128]{1,0:T(8,128)(2,1)} %get-tuple-element.1044), channel_id=1, source_target_pairs={{0,1},{1,2},{2,3},{3,4},{4,5},{5,6},{6,7},{8,9},{9,10},{10,11},{11... | collective-permute-start | bytes 49160 | tf_op jit(solution)/shard_map/while/body/eval_jaxpr/ppermute | solution.py:113
  1093.2 13.3 collective-permute-start
  1122.9 13.3 collective-permute-start
  1139.9 12.1 scatter_custom_fusion.5
  1152.6 13.3 collective-permute-start
  1201.6 14.2 %psum.14 = f32[1]{0:T(128)} all-reduce(f32[1]{0:T(128)} %bitcast.15), channel_id=1, replica_groups=mesh['dp'=4,'stage'=8] {'stage'}, use_global_device_ids=true, to_apply=%region_15.16 | all-reduce | flops 1 | bytes 8 | tf_op jit(solution)/shard_map/psum | solution.py:121
  1215.8 154.5 %all-reduce.2.cloned.1.call-done = f32[30592,128]{1,0:T(8,128)} async-done(((f32[30592,128]{1,0:T(8,128)}), f32[30592,128]{1,0:T(8,128)}) %all-reduce.2.cloned.1.call-update) | async-done | bytes 15663120 | tf_op jit(solution)/shard_map/psum | solution.py:120
  (600 shorter events, 712.8 us)
Async XLA Ops:
  7.2 1363.2 %all-reduce.2.cloned.1.call-start = ((), (), s32[]{:S(2)}) async-start(), calls=%async_computation | async-start | bytes 31326208 | tf_op jit(solution)/shard_map/psum | solution.py:120
  14.2 24.9 %collective-permute-start = (bf16[64,128]{1,0:T(8,128)(2,1)}, bf16[64,128]{1,0:T(8,128)(2,1)S(1)}, u32[]{:S(2)}, u32[]{:S(2)}) collective-permute-start(bf16[64,128]{1,0:T(8,128)(2,1)} %get-tuple-element.1044), channel_id=1, source_target_pairs={{0,1},{1,2},{2,3},{3,4},{4,5},{5,6},{6,7},{8,9},{9,10},{10,11},{11... | collective-permute-start | bytes 49160 | tf_op jit(solution)/shard_map/while/body/eval_jaxpr/ppermute | solution.py:113
  19.0 20.2 %collective-permute-start.1 = (bf16[64,128]{1,0:T(8,128)(2,1)S(1)}, bf16[64,128]{1,0:T(8,128)(2,1)S(1)}, u32[]{:S(2)}, u32[]{:S(2)}) collective-permute-start(bf16[64,128]{1,0:T(8,128)(2,1)S(1)} %get-tuple-element.1049), channel_id=1, source_target_pairs={{1,0},{2,1},{3,2},{4,3},{5,4},{6,5},{7,6},{9,8},{10,9},{11,10},{12... | collective-permute-start | bytes 49160 | tf_op jit(solution)/shard_map/while/body/eval_jaxpr/ppermute | solution.py:114
  96.7 18.5 %collective-permute-start = (bf16[64,128]{1,0:T(8,128)(2,1)}, bf16[64,128]{1,0:T(8,128)(2,1)S(1)}, u32[]{:S(2)}, u32[]{:S(2)}) collective-permute-start(bf16[64,128]{1,0:T(8,128)(2,1)} %get-tuple-element.1044), channel_id=1, source_target_pairs={{0,1},{1,2},{2,3},{3,4},{4,5},{5,6},{6,7},{8,9},{9,10},{10,11},{11... | collective-permute-start | bytes 49160 | tf_op jit(solution)/shard_map/while/body/eval_jaxpr/ppermute | solution.py:113
  122.6 18.5 %collective-permute-start = (bf16[64,128]{1,0:T(8,128)(2,1)}, bf16[64,128]{1,0:T(8,128)(2,1)S(1)}, u32[]{:S(2)}, u32[]{:S(2)}) collective-permute-start(bf16[64,128]{1,0:T(8,128)(2,1)} %get-tuple-element.1044), channel_id=1, source_target_pairs={{0,1},{1,2},{2,3},{3,4},{4,5},{5,6},{6,7},{8,9},{9,10},{10,11},{11... | collective-permute-start | bytes 49160 | tf_op jit(solution)/shard_map/while/body/eval_jaxpr/ppermute | solution.py:113
  148.5 18.5 %collective-permute-start = (bf16[64,128]{1,0:T(8,128)(2,1)}, bf16[64,128]{1,0:T(8,128)(2,1)S(1)}, u32[]{:S(2)}, u32[]{:S(2)}) collective-permute-start(bf16[64,128]{1,0:T(8,128)(2,1)} %get-tuple-element.1044), channel_id=1, source_target_pairs={{0,1},{1,2},{2,3},{3,4},{4,5},{5,6},{6,7},{8,9},{9,10},{10,11},{11... | collective-permute-start | bytes 49160 | tf_op jit(solution)/shard_map/while/body/eval_jaxpr/ppermute | solution.py:113
  174.4 18.5 %collective-permute-start = (bf16[64,128]{1,0:T(8,128)(2,1)}, bf16[64,128]{1,0:T(8,128)(2,1)S(1)}, u32[]{:S(2)}, u32[]{:S(2)}) collective-permute-start(bf16[64,128]{1,0:T(8,128)(2,1)} %get-tuple-element.1044), channel_id=1, source_target_pairs={{0,1},{1,2},{2,3},{3,4},{4,5},{5,6},{6,7},{8,9},{9,10},{10,11},{11... | collective-permute-start | bytes 49160 | tf_op jit(solution)/shard_map/while/body/eval_jaxpr/ppermute | solution.py:113
  200.3 18.5 %collective-permute-start = (bf16[64,128]{1,0:T(8,128)(2,1)}, bf16[64,128]{1,0:T(8,128)(2,1)S(1)}, u32[]{:S(2)}, u32[]{:S(2)}) collective-permute-start(bf16[64,128]{1,0:T(8,128)(2,1)} %get-tuple-element.1044), channel_id=1, source_target_pairs={{0,1},{1,2},{2,3},{3,4},{4,5},{5,6},{6,7},{8,9},{9,10},{10,11},{11... | collective-permute-start | bytes 49160 | tf_op jit(solution)/shard_map/while/body/eval_jaxpr/ppermute | solution.py:113
  252.1 18.5 %collective-permute-start = (bf16[64,128]{1,0:T(8,128)(2,1)}, bf16[64,128]{1,0:T(8,128)(2,1)S(1)}, u32[]{:S(2)}, u32[]{:S(2)}) collective-permute-start(bf16[64,128]{1,0:T(8,128)(2,1)} %get-tuple-element.1044), channel_id=1, source_target_pairs={{0,1},{1,2},{2,3},{3,4},{4,5},{5,6},{6,7},{8,9},{9,10},{10,11},{11... | collective-permute-start | bytes 49160 | tf_op jit(solution)/shard_map/while/body/eval_jaxpr/ppermute | solution.py:113
  278.0 18.5 %collective-permute-start = (bf16[64,128]{1,0:T(8,128)(2,1)}, bf16[64,128]{1,0:T(8,128)(2,1)S(1)}, u32[]{:S(2)}, u32[]{:S(2)}) collective-permute-start(bf16[64,128]{1,0:T(8,128)(2,1)} %get-tuple-element.1044), channel_id=1, source_target_pairs={{0,1},{1,2},{2,3},{3,4},{4,5},{5,6},{6,7},{8,9},{9,10},{10,11},{11... | collective-permute-start | bytes 49160 | tf_op jit(solution)/shard_map/while/body/eval_jaxpr/ppermute | solution.py:113
  303.9 37.2 %collective-permute-start = (bf16[64,128]{1,0:T(8,128)(2,1)}, bf16[64,128]{1,0:T(8,128)(2,1)S(1)}, u32[]{:S(2)}, u32[]{:S(2)}) collective-permute-start(bf16[64,128]{1,0:T(8,128)(2,1)} %get-tuple-element.1044), channel_id=1, source_target_pairs={{0,1},{1,2},{2,3},{3,4},{4,5},{5,6},{6,7},{8,9},{9,10},{10,11},{11... | collective-permute-start | bytes 49160 | tf_op jit(solution)/shard_map/while/body/eval_jaxpr/ppermute | solution.py:113
  348.6 48.5 %collective-permute-start = (bf16[64,128]{1,0:T(8,128)(2,1)}, bf16[64,128]{1,0:T(8,128)(2,1)S(1)}, u32[]{:S(2)}, u32[]{:S(2)}) collective-permute-start(bf16[64,128]{1,0:T(8,128)(2,1)} %get-tuple-element.1044), channel_id=1, source_target_pairs={{0,1},{1,2},{2,3},{3,4},{4,5},{5,6},{6,7},{8,9},{9,10},{10,11},{11... | collective-permute-start | bytes 49160 | tf_op jit(solution)/shard_map/while/body/eval_jaxpr/ppermute | solution.py:113
  404.5 47.7 %collective-permute-start = (bf16[64,128]{1,0:T(8,128)(2,1)}, bf16[64,128]{1,0:T(8,128)(2,1)S(1)}, u32[]{:S(2)}, u32[]{:S(2)}) collective-permute-start(bf16[64,128]{1,0:T(8,128)(2,1)} %get-tuple-element.1044), channel_id=1, source_target_pairs={{0,1},{1,2},{2,3},{3,4},{4,5},{5,6},{6,7},{8,9},{9,10},{10,11},{11... | collective-permute-start | bytes 49160 | tf_op jit(solution)/shard_map/while/body/eval_jaxpr/ppermute | solution.py:113
  459.5 47.7 %collective-permute-start = (bf16[64,128]{1,0:T(8,128)(2,1)}, bf16[64,128]{1,0:T(8,128)(2,1)S(1)}, u32[]{:S(2)}, u32[]{:S(2)}) collective-permute-start(bf16[64,128]{1,0:T(8,128)(2,1)} %get-tuple-element.1044), channel_id=1, source_target_pairs={{0,1},{1,2},{2,3},{3,4},{4,5},{5,6},{6,7},{8,9},{9,10},{10,11},{11... | collective-permute-start | bytes 49160 | tf_op jit(solution)/shard_map/while/body/eval_jaxpr/ppermute | solution.py:113
  514.6 47.7 %collective-permute-start = (bf16[64,128]{1,0:T(8,128)(2,1)}, bf16[64,128]{1,0:T(8,128)(2,1)S(1)}, u32[]{:S(2)}, u32[]{:S(2)}) collective-permute-start(bf16[64,128]{1,0:T(8,128)(2,1)} %get-tuple-element.1044), channel_id=1, source_target_pairs={{0,1},{1,2},{2,3},{3,4},{4,5},{5,6},{6,7},{8,9},{9,10},{10,11},{11... | collective-permute-start | bytes 49160 | tf_op jit(solution)/shard_map/while/body/eval_jaxpr/ppermute | solution.py:113
  569.6 47.7 %collective-permute-start = (bf16[64,128]{1,0:T(8,128)(2,1)}, bf16[64,128]{1,0:T(8,128)(2,1)S(1)}, u32[]{:S(2)}, u32[]{:S(2)}) collective-permute-start(bf16[64,128]{1,0:T(8,128)(2,1)} %get-tuple-element.1044), channel_id=1, source_target_pairs={{0,1},{1,2},{2,3},{3,4},{4,5},{5,6},{6,7},{8,9},{9,10},{10,11},{11... | collective-permute-start | bytes 49160 | tf_op jit(solution)/shard_map/while/body/eval_jaxpr/ppermute | solution.py:113
  618.0 54.4 %collective-permute-start = (bf16[64,128]{1,0:T(8,128)(2,1)}, bf16[64,128]{1,0:T(8,128)(2,1)S(1)}, u32[]{:S(2)}, u32[]{:S(2)}) collective-permute-start(bf16[64,128]{1,0:T(8,128)(2,1)} %get-tuple-element.1044), channel_id=1, source_target_pairs={{0,1},{1,2},{2,3},{3,4},{4,5},{5,6},{6,7},{8,9},{9,10},{10,11},{11... | collective-permute-start | bytes 49160 | tf_op jit(solution)/shard_map/while/body/eval_jaxpr/ppermute | solution.py:113
  673.0 54.4 %collective-permute-start = (bf16[64,128]{1,0:T(8,128)(2,1)}, bf16[64,128]{1,0:T(8,128)(2,1)S(1)}, u32[]{:S(2)}, u32[]{:S(2)}) collective-permute-start(bf16[64,128]{1,0:T(8,128)(2,1)} %get-tuple-element.1044), channel_id=1, source_target_pairs={{0,1},{1,2},{2,3},{3,4},{4,5},{5,6},{6,7},{8,9},{9,10},{10,11},{11... | collective-permute-start | bytes 49160 | tf_op jit(solution)/shard_map/while/body/eval_jaxpr/ppermute | solution.py:113
  703.7 23.7 %collective-permute-start.1 = (bf16[64,128]{1,0:T(8,128)(2,1)S(1)}, bf16[64,128]{1,0:T(8,128)(2,1)S(1)}, u32[]{:S(2)}, u32[]{:S(2)}) collective-permute-start(bf16[64,128]{1,0:T(8,128)(2,1)S(1)} %get-tuple-element.1049), channel_id=1, source_target_pairs={{1,0},{2,1},{3,2},{4,3},{5,4},{6,5},{7,6},{9,8},{10,9},{11,10},{12... | collective-permute-start | bytes 49160 | tf_op jit(solution)/shard_map/while/body/eval_jaxpr/ppermute | solution.py:114
  728.1 47.7 %collective-permute-start = (bf16[64,128]{1,0:T(8,128)(2,1)}, bf16[64,128]{1,0:T(8,128)(2,1)S(1)}, u32[]{:S(2)}, u32[]{:S(2)}) collective-permute-start(bf16[64,128]{1,0:T(8,128)(2,1)} %get-tuple-element.1044), channel_id=1, source_target_pairs={{0,1},{1,2},{2,3},{3,4},{4,5},{5,6},{6,7},{8,9},{9,10},{10,11},{11... | collective-permute-start | bytes 49160 | tf_op jit(solution)/shard_map/while/body/eval_jaxpr/ppermute | solution.py:113
  776.4 54.4 %collective-permute-start = (bf16[64,128]{1,0:T(8,128)(2,1)}, bf16[64,128]{1,0:T(8,128)(2,1)S(1)}, u32[]{:S(2)}, u32[]{:S(2)}) collective-permute-start(bf16[64,128]{1,0:T(8,128)(2,1)} %get-tuple-element.1044), channel_id=1, source_target_pairs={{0,1},{1,2},{2,3},{3,4},{4,5},{5,6},{6,7},{8,9},{9,10},{10,11},{11... | collective-permute-start | bytes 49160 | tf_op jit(solution)/shard_map/while/body/eval_jaxpr/ppermute | solution.py:113
  831.4 54.4 %collective-permute-start = (bf16[64,128]{1,0:T(8,128)(2,1)}, bf16[64,128]{1,0:T(8,128)(2,1)S(1)}, u32[]{:S(2)}, u32[]{:S(2)}) collective-permute-start(bf16[64,128]{1,0:T(8,128)(2,1)} %get-tuple-element.1044), channel_id=1, source_target_pairs={{0,1},{1,2},{2,3},{3,4},{4,5},{5,6},{6,7},{8,9},{9,10},{10,11},{11... | collective-permute-start | bytes 49160 | tf_op jit(solution)/shard_map/while/body/eval_jaxpr/ppermute | solution.py:113
  862.1 23.7 %collective-permute-start.1 = (bf16[64,128]{1,0:T(8,128)(2,1)S(1)}, bf16[64,128]{1,0:T(8,128)(2,1)S(1)}, u32[]{:S(2)}, u32[]{:S(2)}) collective-permute-start(bf16[64,128]{1,0:T(8,128)(2,1)S(1)} %get-tuple-element.1049), channel_id=1, source_target_pairs={{1,0},{2,1},{3,2},{4,3},{5,4},{6,5},{7,6},{9,8},{10,9},{11,10},{12... | collective-permute-start | bytes 49160 | tf_op jit(solution)/shard_map/while/body/eval_jaxpr/ppermute | solution.py:114
  886.5 47.7 %collective-permute-start = (bf16[64,128]{1,0:T(8,128)(2,1)}, bf16[64,128]{1,0:T(8,128)(2,1)S(1)}, u32[]{:S(2)}, u32[]{:S(2)}) collective-permute-start(bf16[64,128]{1,0:T(8,128)(2,1)} %get-tuple-element.1044), channel_id=1, source_target_pairs={{0,1},{1,2},{2,3},{3,4},{4,5},{5,6},{6,7},{8,9},{9,10},{10,11},{11... | collective-permute-start | bytes 49160 | tf_op jit(solution)/shard_map/while/body/eval_jaxpr/ppermute | solution.py:113
  934.8 54.4 %collective-permute-start = (bf16[64,128]{1,0:T(8,128)(2,1)}, bf16[64,128]{1,0:T(8,128)(2,1)S(1)}, u32[]{:S(2)}, u32[]{:S(2)}) collective-permute-start(bf16[64,128]{1,0:T(8,128)(2,1)} %get-tuple-element.1044), channel_id=1, source_target_pairs={{0,1},{1,2},{2,3},{3,4},{4,5},{5,6},{6,7},{8,9},{9,10},{10,11},{11... | collective-permute-start | bytes 49160 | tf_op jit(solution)/shard_map/while/body/eval_jaxpr/ppermute | solution.py:113
  989.8 54.4 %collective-permute-start = (bf16[64,128]{1,0:T(8,128)(2,1)}, bf16[64,128]{1,0:T(8,128)(2,1)S(1)}, u32[]{:S(2)}, u32[]{:S(2)}) collective-permute-start(bf16[64,128]{1,0:T(8,128)(2,1)} %get-tuple-element.1044), channel_id=1, source_target_pairs={{0,1},{1,2},{2,3},{3,4},{4,5},{5,6},{6,7},{8,9},{9,10},{10,11},{11... | collective-permute-start | bytes 49160 | tf_op jit(solution)/shard_map/while/body/eval_jaxpr/ppermute | solution.py:113
  1020.5 23.7 %collective-permute-start.1 = (bf16[64,128]{1,0:T(8,128)(2,1)S(1)}, bf16[64,128]{1,0:T(8,128)(2,1)S(1)}, u32[]{:S(2)}, u32[]{:S(2)}) collective-permute-start(bf16[64,128]{1,0:T(8,128)(2,1)S(1)} %get-tuple-element.1049), channel_id=1, source_target_pairs={{1,0},{2,1},{3,2},{4,3},{5,4},{6,5},{7,6},{9,8},{10,9},{11,10},{12... | collective-permute-start | bytes 49160 | tf_op jit(solution)/shard_map/while/body/eval_jaxpr/ppermute | solution.py:114
  1044.9 47.7 %collective-permute-start = (bf16[64,128]{1,0:T(8,128)(2,1)}, bf16[64,128]{1,0:T(8,128)(2,1)S(1)}, u32[]{:S(2)}, u32[]{:S(2)}) collective-permute-start(bf16[64,128]{1,0:T(8,128)(2,1)} %get-tuple-element.1044), channel_id=1, source_target_pairs={{0,1},{1,2},{2,3},{3,4},{4,5},{5,6},{6,7},{8,9},{9,10},{10,11},{11... | collective-permute-start | bytes 49160 | tf_op jit(solution)/shard_map/while/body/eval_jaxpr/ppermute | solution.py:113
  1093.2 29.1 %collective-permute-start = (bf16[64,128]{1,0:T(8,128)(2,1)}, bf16[64,128]{1,0:T(8,128)(2,1)S(1)}, u32[]{:S(2)}, u32[]{:S(2)}) collective-permute-start(bf16[64,128]{1,0:T(8,128)(2,1)} %get-tuple-element.1044), channel_id=1, source_target_pairs={{0,1},{1,2},{2,3},{3,4},{4,5},{5,6},{6,7},{8,9},{9,10},{10,11},{11... | collective-permute-start | bytes 49160 | tf_op jit(solution)/shard_map/while/body/eval_jaxpr/ppermute | solution.py:113
  1122.9 29.0 %collective-permute-start = (bf16[64,128]{1,0:T(8,128)(2,1)}, bf16[64,128]{1,0:T(8,128)(2,1)S(1)}, u32[]{:S(2)}, u32[]{:S(2)}) collective-permute-start(bf16[64,128]{1,0:T(8,128)(2,1)} %get-tuple-element.1044), channel_id=1, source_target_pairs={{0,1},{1,2},{2,3},{3,4},{4,5},{5,6},{6,7},{8,9},{9,10},{10,11},{11... | collective-permute-start | bytes 49160 | tf_op jit(solution)/shard_map/while/body/eval_jaxpr/ppermute | solution.py:113
  1152.6 29.0 %collective-permute-start = (bf16[64,128]{1,0:T(8,128)(2,1)}, bf16[64,128]{1,0:T(8,128)(2,1)S(1)}, u32[]{:S(2)}, u32[]{:S(2)}) collective-permute-start(bf16[64,128]{1,0:T(8,128)(2,1)} %get-tuple-element.1044), channel_id=1, source_target_pairs={{0,1},{1,2},{2,3},{3,4},{4,5},{5,6},{6,7},{8,9},{9,10},{10,11},{11... | collective-permute-start | bytes 49160 | tf_op jit(solution)/shard_map/while/body/eval_jaxpr/ppermute | solution.py:113
  1182.3 18.5 %collective-permute-start = (bf16[64,128]{1,0:T(8,128)(2,1)}, bf16[64,128]{1,0:T(8,128)(2,1)S(1)}, u32[]{:S(2)}, u32[]{:S(2)}) collective-permute-start(bf16[64,128]{1,0:T(8,128)(2,1)} %get-tuple-element.1044), channel_id=1, source_target_pairs={{0,1},{1,2},{2,3},{3,4},{4,5},{5,6},{6,7},{8,9},{9,10},{10,11},{11... | collective-permute-start | bytes 49160 | tf_op jit(solution)/shard_map/while/body/eval_jaxpr/ppermute | solution.py:113
  (33 other events, 480.2 us)
Sparse Core Ops, SparseCore 0:
  1201.0 169.2 all-reduce.1
where the time goes:
time: 1400 us; the launch traced here: 1390 us
  starting transfers between devices  603 us (43%)
  other arithmetic  408 us (29%)
  waiting for transfers between devices  210 us (15%)
  local copies, waits for them, and re-layouts  104 us (7%)
  matrix products  28.9 us (2%)
  blocking collectives  14.2 us (1%)
  between operations  14.2 us (1%)
    ppermute x30, starting transfers between devices, tick(): recv_act = lax.ppermute(y_out, 'stage', fwd_perm)  539 us
    scatter-add x30, other arithmetic, tick(): grad_emb = grad_emb.at[tok_b].add(emb_rows)  363 us
    psum x1, waiting for transfers between devices, device_fn(): grad_emb = lax.psum(final_state[7], 'stage')  155 us
    gather x16, local copies, waits for them, and re-layouts, tick(): x_in = jnp.where(is_first, jnp.take(emb_table, tok_f, axis=0), recv_act)  77.3 us
    ppermute x30, starting transfers between devices, tick(): recv_grad = lax.ppermute(grad_in, 'stage', bwd_perm)  64.5 us
    ppermute x30, waiting for transfers between devices, tick(): recv_grad = lax.ppermute(grad_in, 'stage', bwd_perm)  55.4 us
  transfers between devices with their start and end apart: 61, of which 16 were waited for; matrix products, arithmetic and copies ran while one was open for 29% of the time, Pallas kernels for 0%

commit v1 on v0

v1 whole, which is shorter than its diff:
```python
import functools
import math

import jax
import jax.numpy as jnp
from jax import lax
from jax.experimental import pallas as pl
from jax.experimental.pallas import tpu as pltpu
from jax.sharding import PartitionSpec as P

MESH = pl.DeviceIdType.MESH
F32 = jnp.float32
BF16 = jnp.bfloat16
LOG2E = math.log2(math.e)
LN2 = math.log(2.0)
GELU_C = math.sqrt(2.0 / math.pi)
HEAD_BLOCK = 2048
EMB_BLOCK = 512
VMEM_BYTES = 60 * 1024 * 1024


def dot_nn(a, b):
    return lax.dot_general(a, b, (((1,), (0,)), ((), ())), preferred_element_type=F32)


def dot_nt(a, b):
    return lax.dot_general(a, b, (((1,), (1,)), ((), ())), preferred_element_type=F32)


def dot_tn(a, b):
    return lax.dot_general(a, b, (((0,), (0,)), ((), ())), preferred_element_type=F32)


def gelu_value(a):
    return a * (0.5 * (1.0 + jnp.tanh(GELU_C * (a + 0.044715 * (a * a * a)))))


def gelu_slope(a):
    sq = a * a
    t = jnp.tanh(GELU_C * (a + 0.044715 * (sq * a)))
    return 0.5 * (1.0 + t) + (0.5 * a) * (1.0 - t * t) * (GELU_C * (1.0 + (3.0 * 0.044715) * sq))


def column_of(row, size):
    return jnp.transpose(jnp.broadcast_to(row, (size, size)))


def row_of(col, size):
    eye = lax.broadcasted_iota(jnp.int32, (size, size), 0) == lax.broadcasted_iota(jnp.int32, (size, size), 1)
    return jnp.sum(jnp.where(eye, jnp.broadcast_to(col, (size, size)), 0.0), axis=0, keepdims=True)


def token_kernel(
    n_stage, tok_ref, lab_ref, emb_hbm, wup_hbm, wdn_hbm,
    n_out, st_out, xs_out, gs_out, dx_out, ids_out, starts_out,
    wup, wdn, emb, z_buf, xs, gs, pre, n_loc, st_loc, gat,
    loc_sem, wsend, upr, dnr, xsend, xrecv, gsend, grecv, nsend, nrecv, ssend, srecv, dsend, drecv,
):
    me = lax.axis_index("stage")
    n_chip = n_stage // 2
    chip, core = me // 2, lax.rem(me, 2)
    sib = chip * 2 + (1 - core)
    right = lax.rem(chip + 1, n_chip) * 2 + core
    left = lax.rem(chip + n_chip - 1, n_chip) * 2 + core
    far = lax.rem(chip + 2, n_chip) * 2 + core
    peers = [lax.rem(me + d, n_stage) for d in range(1, n_stage)]
    tok_n, dim = n_loc.shape
    vocab = emb.shape[0]
    total = n_stage * tok_n
    scale = dim ** -0.5

    load_up = pltpu.make_async_copy(wup_hbm, wup.at[me], loc_sem.at[0])
    load_dn = pltpu.make_async_copy(wdn_hbm, wdn.at[me], loc_sem.at[1])
    load_emb = pltpu.make_async_copy(emb_hbm, emb, loc_sem.at[2])
    load_up.start()
    load_dn.start()
    load_emb.start()

    barrier = pltpu.get_barrier_semaphore()
    for peer in peers:
        pl.semaphore_signal(barrier, inc=1, device_id={"stage": peer}, device_id_type=MESH)
    pl.semaphore_wait(barrier, n_stage - 1)
    load_up.wait()
    load_dn.wait()

    def up_copy(i, slot, dst):
        return pltpu.make_async_remote_copy(
            wup.at[slot], wup.at[slot], wsend.at[i], upr.at[slot], device_id={"stage": dst}, device_id_type=MESH)

    def dn_copy(i, slot, dst):
        return pltpu.make_async_remote_copy(
            wdn.at[slot], wdn.at[slot], wsend.at[i], dnr.at[slot], device_id={"stage": dst}, device_id_type=MESH)

    first = [up_copy(0, me, right), dn_copy(1, me, left), dn_copy(2, me, right), up_copy(3, me, left),
             up_copy(4, me, sib), dn_copy(5, me, sib)]
    for copy in first:
        copy.start()

    tok_row = tok_ref[...]
    pos = lax.broadcasted_iota(jnp.int32, (n_stage, tok_n), 0) * tok_n + lax.broadcasted_iota(jnp.int32, (n_stage, tok_n), 1)
    key_row = tok_row * total + pos
    lane = lax.broadcasted_iota(jnp.int32, (tok_n, tok_n), 1)
    key_cols = [column_of(key_row[j:j + 1, :], tok_n) for j in range(n_stage)]
    tok_cols = [column_of(tok_row[j:j + 1, :], tok_n) for j in range(n_stage)]
    rank_rows = []
    for i in range(n_stage):
        acc = jnp.zeros((tok_n, tok_n), jnp.int32)
        for j in range(n_stage):
            acc = acc + jnp.where(key_cols[j] < key_row[i:i + 1, :], 1, 0)
        rank_rows.append(jnp.sum(acc, axis=0, keepdims=True))
    rank_cols = [column_of(r, tok_n) for r in rank_rows]
    for c in range(n_stage):
        acc = jnp.zeros((tok_n, tok_n), jnp.int32)
        for j in range(n_stage):
            acc = acc + jnp.where(rank_cols[j] == lane + c * tok_n, tok_cols[j], 0)
        ids_out[c] = jnp.broadcast_to(jnp.sum(acc, axis=0, keepdims=True), (8, tok_n))
    acc = jnp.zeros((tok_n, tok_n), jnp.int32)
    for j in range(n_stage):
        acc = acc + jnp.where(tok_cols[j] < lane * EMB_BLOCK, 1, 0)
    starts_out[0:8, :] = jnp.broadcast_to(jnp.sum(acc, axis=0, keepdims=True), (8, tok_n))
    for i in range(n_stage):
        starts_out[8 + i:9 + i, :] = rank_rows[i]

    load_emb.wait()
    pick = jnp.concatenate(
        [column_of(tok_ref[pl.ds(me, 1), :], tok_n), column_of(lab_ref[pl.ds(me, 1), :], tok_n)], axis=0)
    lane2 = lax.broadcasted_iota(jnp.int32, (2 * tok_n, tok_n), 1)

    def blocks(body):
        full = vocab // HEAD_BLOCK

        def step(i, carry):
            body(pl.multiple_of(i * HEAD_BLOCK, HEAD_BLOCK), HEAD_BLOCK)
            return carry

        lax.fori_loop(0, full, step, 0)
        if vocab % HEAD_BLOCK:
            body(full * HEAD_BLOCK, vocab % HEAD_BLOCK)

    gat[...] = jnp.zeros_like(gat)

    def gather_block(v0, size):
        hot = jnp.concatenate(
            [jnp.where(pick == lane2 + (v0 + j * tok_n), 1.0, 0.0).astype(BF16) for j in range(size // tok_n)], axis=1)
        gat[...] += dot_nn(hot, emb[pl.ds(v0, size), :])

    blocks(gather_block)
    x0 = gat[0:tok_n, :].astype(BF16)
    lab_rows = gat[tok_n:2 * tok_n, :]
    lab_bf = lab_rows.astype(BF16)

    up_copy(0, left, sib).wait_recv()
    second = [up_copy(6, left, right), up_copy(7, left, sib)]
    second[0].start()
    second[1].start()
    dn_copy(0, right, sib).wait_recv()
    second += [dn_copy(8, right, left), dn_copy(9, right, sib)]
    second[2].start()
    second[3].start()
    dn_copy(0, left, sib).wait_recv()
    second.append(dn_copy(10, left, sib))
    second[4].start()
    up_copy(0, right, sib).wait_recv()
    second.append(up_copy(11, right, sib))
    second[5].start()
    up_copy(0, far, sib).wait_recv()
    second.append(up_copy(12, far, sib))
    second[6].start()
    dn_copy(0, far, sib).wait_recv()
    second.append(dn_copy(13, far, sib))
    second[7].start()

    def x_copy(layer):
        return pltpu.make_async_remote_copy(
            xs.at[layer], xs_out.at[me], xsend.at[layer], xrecv.at[me], device_id={"stage": layer}, device_id_type=MESH)

    def g_copy(layer):
        return pltpu.make_async_remote_copy(
            gs.at[layer + 1], gs_out.at[me], gsend.at[layer], grecv.at[me], device_id={"stage": layer}, device_id_type=MESH)

    own_x = pltpu.make_async_copy(xs.at[me], xs_out.at[me], loc_sem.at[0])
    own_g = pltpu.make_async_copy(gs.at[me + 1], gs_out.at[me], loc_sem.at[1])

    xs[0] = x0

    def forward(layer, carry):
        @pl.when(lax.rem(layer, 2) != core)
        def _():
            up_copy(0, layer, sib).wait_recv()
            dn_copy(0, layer, sib).wait_recv()

        x = xs[layer]
        a = dot_nn(x, wup[layer]).astype(BF16)
        pre[layer] = a
        h = gelu_value(a.astype(F32)).astype(BF16)
        xs[layer + 1] = (x.astype(F32) + dot_nn(h, wdn[layer])).astype(BF16)

        @pl.when(layer != me)
        def _():
            x_copy(layer).start()

        @pl.when(layer == me)
        def _():
            own_x.start()

        return carry

    lax.fori_loop(0, n_stage, forward, 0)

    x_last = xs[n_stage].astype(F32)
    inv = lax.rsqrt(jnp.mean(x_last * x_last, axis=-1, keepdims=True) + 1e-6)
    n_val = (x_last * inv).astype(BF16)
    n_loc[...] = n_val

    def spread(src, dst, send, recv):
        return [pltpu.make_async_remote_copy(src, dst.at[me], send.at[d], recv.at[me], device_id={"stage": peer},
                                             device_id_type=MESH) for d, peer in enumerate(peers)]

    def stat_block(v0, size):
        z = (dot_nt(n_loc[...], emb[pl.ds(v0, size), :]) * scale).astype(BF16)
        z_buf[:, pl.ds(v0, size)] = z
        parts = [z[:, j * tok_n:(j + 1) * tok_n].astype(F32) for j in range(size // tok_n)]
        m_old = gat[0:tok_n, :]
        m_new = functools.reduce(jnp.maximum, parts, m_old)
        s_new = gat[tok_n:2 * tok_n, :] * jnp.exp2((m_old - m_new) * LOG2E)
        for part in parts:
            s_new = s_new + jnp.exp2((part - m_new) * LOG2E)
        gat[0:tok_n, :] = m_new
        gat[tok_n:2 * tok_n, :] = s_new

    gat[0:tok_n, :] = jnp.full((tok_n, dim), -1e30, F32)
    gat[tok_n:2 * tok_n, :] = jnp.zeros((tok_n, dim), F32)
    send_n = spread(n_loc, n_out, nsend, nrecv)
    for copy in send_n:
        copy.start()
    own_n = pltpu.make_async_copy(n_loc, n_out.at[me], loc_sem.at[2])
    own_n.start()
    blocks(stat_block)
    m_lane = gat[0:tok_n, :]
    m_tok = jnp.max(m_lane, axis=-1, keepdims=True)
    s_tok = jnp.sum(gat[tok_n:2 * tok_n, :] * jnp.exp2((m_lane - m_tok) * LOG2E), axis=-1, keepdims=True)
    lse = m_tok + jnp.log(s_tok)
    level = lse * LOG2E + math.log2(total)
    z_pair = (dot_nt(n_val, lab_bf) * scale).astype(BF16).astype(F32)
    eye = lax.broadcasted_iota(jnp.int32, (tok_n, tok_n), 0) == lane
    z_lab = jnp.sum(jnp.where(eye, z_pair, 0.0), axis=-1, keepdims=True)
    p_lab = jnp.exp2(z_lab * LOG2E - level)
    d_lab = (p_lab - 1.0 / total).astype(BF16).astype(F32)
    p_lab = p_lab.astype(BF16).astype(F32)
    st_loc[...] = jnp.concatenate(
        [row_of(level, tok_n), row_of(d_lab, tok_n), row_of(lse - z_lab, tok_n), jnp.zeros((5, tok_n), F32)], axis=0)
    level_full = jnp.broadcast_to(level, (tok_n, tok_n))

    gat[0:tok_n, :] = (d_lab - p_lab) * lab_rows
    send_s = spread(st_loc, st_out, ssend, srecv)
    for copy in send_s:
        copy.start()
    own_s = pltpu.make_async_copy(st_loc, st_out.at[me], loc_sem.at[3])
    own_s.start()

    def grad_block(v0, size):
        parts = []
        for j in range(size // tok_n):
            z = z_buf[:, pl.ds(v0 + j * tok_n, tok_n)].astype(F32)
            parts.append(jnp.exp2(z * LOG2E - level_full).astype(BF16))
        gat[0:tok_n, :] += dot_nn(jnp.concatenate(parts, axis=1), emb[pl.ds(v0, size), :])

    blocks(grad_block)
    dn = (gat[0:tok_n, :] * scale).astype(BF16).astype(F32)
    corr = jnp.mean(dn * x_last, axis=-1, keepdims=True)
    gs[n_stage] = (inv * dn - x_last * (inv * inv * inv * corr)).astype(BF16)

    def backward(i, carry):
        layer = n_stage - 1 - i
        g = gs[layer + 1]
        dh = dot_nt(g, wdn[layer]).astype(BF16).astype(F32)
        da = (dh * gelu_slope(pre[layer].astype(F32))).astype(BF16)
        gs[layer] = (g.astype(F32) + dot_nt(da, wup[layer])).astype(BF16)

        @pl.when(layer != me)
        def _():
            g_copy(layer).start()

        @pl.when(layer == me)
        def _():
            own_g.start()

        return carry

    lax.fori_loop(0, n_stage, backward, 0)
    send_d = spread(gs.at[0], dx_out, dsend, drecv)
    for copy in send_d:
        copy.start()
    own_d = pltpu.make_async_copy(gs.at[0], dx_out.at[me], loc_sem.at[4])
    own_d.start()

    for copy in first + second + send_n + send_s:
        copy.wait_send()
    for copy in (own_x, own_g, own_n, own_s, own_d):
        copy.wait()
    for d, peer in enumerate(peers):
        pltpu.make_async_remote_copy(xs.at[peer], xs_out.at[peer], xsend.at[peer], xrecv.at[peer],
                                     device_id={"stage": peer}, device_id_type=MESH).wait()
        pltpu.make_async_remote_copy(gs.at[peer + 1], gs_out.at[peer], gsend.at[peer], grecv.at[peer],
                                     device_id={"stage": peer}, device_id_type=MESH).wait()
        for src, dst, send, recv in ((n_loc, n_out, nsend, nrecv), (st_loc, st_out, ssend, srecv)):
            pltpu.make_async_remote_copy(src, dst.at[peer], send.at[d], recv.at[peer],
                                         device_id={"stage": peer}, device_id_type=MESH).wait_recv()
        pltpu.make_async_remote_copy(gs.at[0], dx_out.at[peer], dsend.at[d], drecv.at[peer],
                                     device_id={"stage": peer}, device_id_type=MESH).wait_recv()
    for copy in send_d:
        copy.wait_send()


def weight_kernel(x_ref, g_ref, wup_ref, wdn_ref, st_ref, gup_ref, gdn_ref, loss_ref):
    n_stage, tok_n, _ = x_ref.shape
    step = 2

    def body(i, carry):
        x = jnp.concatenate([x_ref[step * i + k] for k in range(step)], axis=0)
        g = jnp.concatenate([g_ref[step * i + k] for k in range(step)], axis=0)
        a = dot_nn(x, wup_ref[...]).astype(BF16).astype(F32)
        sq = a * a
        t = jnp.tanh(GELU_C * (a + 0.044715 * (sq * a)))
        cdf = 0.5 * (1.0 + t)
        h = (a * cdf).astype(BF16)
        slope = cdf + (0.5 * a) * (1.0 - t * t) * (GELU_C * (1.0 + (3.0 * 0.044715) * sq))
        dh = dot_nt(g, wdn_ref[...]).astype(BF16).astype(F32)
        da = (dh * slope).astype(BF16)
        gup_ref[...] += dot_tn(x, da)
        gdn_ref[...] += dot_tn(h, g)
        return carry

    gup_ref[...] = jnp.zeros_like(gup_ref)
    gdn_ref[...] = jnp.zeros_like(gdn_ref)
    lax.fori_loop(0, n_stage // step, body, 0)
    nll = jnp.sum(st_ref[:, 2, :], keepdims=True) * (1.0 / (n_stage * tok_n))
    loss_ref[...] = jnp.broadcast_to(nll, loss_ref.shape)


def table_kernel(starts_sm, emb_ref, n_ref, st_ref, lab_ref, dx_ref, ids_ref, rank_ref, out_ref, n_t, level, d_lab, lab16, dxs):
    n_chunk, tok_n, dim = n_ref.shape
    total = n_chunk * tok_n
    blk = pl.program_id(0)
    rows = out_ref.shape[0]
    scale = dim ** -0.5

    @pl.when(blk == 0)
    def _():
        row_id = lax.broadcasted_iota(jnp.int32, (tok_n, tok_n), 0)
        for i in range(n_chunk):
            cols = slice(i * tok_n, (i + 1) * tok_n)
            n_t[:, cols] = jnp.transpose(n_ref[i])
            level[:, cols] = jnp.broadcast_to(st_ref[i, 0:1, :], (8, tok_n))
            d_lab[:, cols] = jnp.broadcast_to(st_ref[i, 1:2, :], (16, tok_n)).astype(BF16)
        for c in range(n_chunk):
            acc = jnp.zeros((tok_n, dim), F32)
            for i in range(n_chunk):
                hot = jnp.where(rank_ref[i:i + 1, :] == row_id + c * tok_n, 1.0, 0.0).astype(BF16)
                acc = acc + dot_nn(hot, dx_ref[i])
            dxs[c] = acc.astype(BF16)

    wide = 2 * tok_n
    e = emb_ref[...]
    base = blk * rows
    acc = jnp.zeros((rows, dim), F32)
    row16 = lax.broadcasted_iota(jnp.int16, (rows, wide), 0)
    for t in range(total // wide):
        cols = slice(t * wide, (t + 1) * wide)
        z = (dot_nn(e, n_t[:, cols]) * scale).astype(BF16).astype(F32)
        p = jnp.exp2(z * LOG2E - level[0:1, cols]).astype(BF16)
        lab = jnp.concatenate([lab_ref[2 * t:2 * t + 1, :], lab_ref[2 * t + 1:2 * t + 2, :]], axis=1) - base
        lab = jnp.broadcast_to(lab, (16, wide)).astype(jnp.int16)
        dz = jnp.where(row16 == lab[0:1, :], d_lab[0:1, cols], p)
        nn = jnp.concatenate([n_ref[2 * t], n_ref[2 * t + 1]], axis=0)
        acc = acc + dot_nn(dz, nn)

    row32 = lax.broadcasted_iota(jnp.int32, (rows, tok_n), 0)

    def token_term(c):
        hot = jnp.where(row32 == ids_ref[c, 0:1, :] - base, 1.0, 0.0).astype(BF16)
        return dot_nn(hot, dxs[c])

    first = jnp.minimum(starts_sm[blk] // tok_n, n_chunk - 1)
    last = (starts_sm[blk + 1] + tok_n - 1) // tok_n
    out_ref[...] = acc * scale + token_term(first)

    def more(c, carry):
        out_ref[...] += token_term(c)
        return carry

    lax.fori_loop(first + 1, last, more, 0)


def solution(mesh):
    n_stage = mesh.shape["stage"]

    def device_fn(tokens, labels, emb_table, w_up, w_down):
        vocab, dim = emb_table.shape
        ffn = w_up.shape[2]
        total = tokens.shape[0] * tokens.shape[1]
        tok_n = total // n_stage
        tok8 = tokens.reshape(n_stage, tok_n)
        lab8 = labels.reshape(n_stage, tok_n)
        w_up, w_down = w_up[0], w_down[0]
        vmem = pl.BlockSpec(memory_space=pltpu.VMEM)
        hbm = pl.BlockSpec(memory_space=pl.ANY)
        dma = pltpu.SemaphoreType.DMA
        n_blk = pl.cdiv(vocab, EMB_BLOCK)
        act = jax.ShapeDtypeStruct((n_stage, tok_n, dim), BF16)
        n_all, st_all, xs_all, gs_all, dx_all, ids, starts = pl.pallas_call(
            functools.partial(token_kernel, n_stage),
            out_shape=[act, jax.ShapeDtypeStruct((n_stage, 8, tok_n), F32), act, act, act,
                       jax.ShapeDtypeStruct((n_stage, 8, tok_n), jnp.int32),
                       jax.ShapeDtypeStruct((8 + n_stage, tok_n), jnp.int32)],
            in_specs=[vmem, vmem, hbm, hbm, hbm],
            out_specs=[hbm, hbm, hbm, hbm, hbm, vmem, vmem],
            scratch_shapes=[
                pltpu.VMEM((n_stage, dim, ffn), BF16), pltpu.VMEM((n_stage, ffn, dim), BF16),
                pltpu.VMEM((vocab, dim), BF16), pltpu.VMEM((tok_n, vocab), BF16),
                pltpu.VMEM((n_stage + 1, tok_n, dim), BF16), pltpu.VMEM((n_stage + 1, tok_n, dim), BF16),
                pltpu.VMEM((n_stage, tok_n, ffn), BF16), pltpu.VMEM((tok_n, dim), BF16),
                pltpu.VMEM((8, tok_n), F32), pltpu.VMEM((2 * tok_n, dim), F32),
                dma((5,)), dma((14,))] + [dma((n_stage,))] * 12,
            compiler_params=pltpu.CompilerParams(collective_id=0, has_side_effects=True, vmem_limit_bytes=VMEM_BYTES),
            name="token_pass",
        )(tok8, lab8, emb_table, w_up, w_down)

        grad_up, grad_down, loss = pl.pallas_call(
            weight_kernel,
            out_shape=[jax.ShapeDtypeStruct((dim, ffn), F32), jax.ShapeDtypeStruct((ffn, dim), F32),
                       jax.ShapeDtypeStruct((8, 128), F32)],
            in_specs=[vmem] * 5, out_specs=[vmem] * 3,
            compiler_params=pltpu.CompilerParams(vmem_limit_bytes=VMEM_BYTES),
            name="weight_grads",
        )(xs_all, gs_all, w_up, w_down, st_all)

        whole3 = lambda i, s: (0, 0, 0)
        whole2 = lambda i, s: (0, 0)
        grad_emb = pl.pallas_call(
            table_kernel,
            grid_spec=pltpu.PrefetchScalarGridSpec(
                num_scalar_prefetch=1, grid=(n_blk,),
                in_specs=[pl.BlockSpec((EMB_BLOCK, dim), lambda i, s: (i, 0)),
                          pl.BlockSpec((n_stage, tok_n, dim), whole3), pl.BlockSpec((n_stage, 8, tok_n), whole3),
                          pl.BlockSpec((n_stage, tok_n), whole2), pl.BlockSpec((n_stage, tok_n, dim), whole3),
                          pl.BlockSpec((n_stage, 8, tok_n), whole3), pl.BlockSpec((n_stage, tok_n), whole2)],
                out_specs=pl.BlockSpec((EMB_BLOCK, dim), lambda i, s: (i, 0)),
                scratch_shapes=[pltpu.VMEM((dim, total), BF16), pltpu.VMEM((8, total), F32), pltpu.VMEM((16, total), BF16),
                                pltpu.VMEM((16, total), jnp.int16), pltpu.VMEM((n_stage, tok_n, dim), BF16)]),
            out_shape=jax.ShapeDtypeStruct((vocab, dim), F32),
            compiler_params=pltpu.CompilerParams(dimension_semantics=("arbitrary",), vmem_limit_bytes=VMEM_BYTES),
            name="table_grad",
        )(starts[0], emb_table, n_all, st_all, lab8, dx_all, ids, starts[8:])
        return loss[0, :1], grad_up[None], grad_down[None], grad_emb

    return jax.shard_map(
        device_fn, mesh=mesh,
        in_specs=(P("dp", None), P("dp", None), P(None, None), P("stage", None, None), P("stage", None, None)),
        out_specs=(P("dp"), P(("dp", "stage"), None, None), P(("dp", "stage"), None, None), P("dp", None)),
        check_vma=False)
```

time: 1400 us -> 124 us (0.09)
  starting transfers between devices: 603 us -> 0 us
  other arithmetic: 408 us -> 0 us
  waiting for transfers between devices: 210 us -> 0 us
  Pallas kernels: 0 us -> 116 us
  local copies, waits for them, and re-layouts: 104 us -> 6.36 us
  matrix products: 28.9 us -> 0 us
  blocking collectives: 14.2 us -> 0 us
    ppermute x60 -> x0, starting transfers between devices: 603 us -> none  [the longest x30 539 us: tick(): recv_act = lax.ppermute(y_out, 'stage', fwd_perm)]
    scatter-add x30 -> x0, other arithmetic: 363 us -> none  [tick(): grad_emb = grad_emb.at[tok_b].add(emb_rows)]
    psum x1 -> x0, waiting for transfers between devices: 155 us -> none  [device_fn(): grad_emb = lax.psum(final_state[7], 'stage')]
    pallas_call x0 -> x3, Pallas kernels: none -> 116 us  [the longest x1 64.5 us: device_fn(): pl.pallas_call(table_kernel, grid_spec=pltpu.PrefetchScalarGridSpec(num_s...]
    gather x16 -> x0, local copies, waits for them, and re-layouts: 77.3 us -> none  [tick(): x_in = jnp.where(is_first, jnp.take(emb_table, tok_f, axis=0), recv_act)]
    ppermute x60 -> x0, waiting for transfers between devices: 55.4 us -> none  [the longest x30 55.4 us: tick(): recv_grad = lax.ppermute(grad_in, 'stage', bwd_perm)]
    select_n x62 -> x0, other arithmetic: 32.3 us -> none  [the longest x30 21 us: tick(): grad_emb = grad_emb.at[tok_b].add(emb_rows)]
    dot_general x96 -> x0, matrix products: 28.9 us -> none  [the longest x16 12.8 us: block_forward(): branch = jnp.dot(hidden, w_down, preferred_element_type=jnp.float32)]
  transfers between devices with their start and end apart: 61 -> 0, of which waited for: 16 -> 0; matrix products, arithmetic and copies ran while one was open for 29% -> 0% of each run, Pallas kernels for 0% -> 0%
where the time goes in v1:
time: 124 us; the launch traced here: 123 us
  Pallas kernels  116 us (94%)
  local copies, waits for them, and re-layouts  6.36 us (5%)
    pallas_call x1, Pallas kernels, device_fn(): pl.pallas_call(table_kernel, grid_spec=pltpu.PrefetchScalarGridSpec(num_s...  64.5 us
    pallas_call x1, Pallas kernels, device_fn(): pl.pallas_call(functools.partial(token_kernel, n_stage), out_shape=[act,...  46.5 us
    pallas_call x1, Pallas kernels, device_fn(): pl.pallas_call(weight_kernel, out_shape=[jax.ShapeDtypeStruct((dim, ffn),...  4.85 us

profile of v1, /device:TPU:81, one launch (start us, length us, event | category | flops | bytes accessed | tf_op | source)
XLA Modules:
  0.0 122.9 jit_solution(11409017172327584121)
XLA Ops:
  0.6 1.4 %reshape.15.lab_ref = s32[8,128]{1,0:T(8,128)} reshape(s32[16,64]{1,0:T(8,128)} %param.6) | data formatting | bytes 8192 | tf_op jit(solution)/shard_map/reshape | solution.py:404
  2.0 1.4 %reshape.14.tok_ref = s32[8,128]{1,0:T(8,128)} reshape(s32[16,64]{1,0:T(8,128)} %param.5) | data formatting | bytes 8192 | tf_op jit(solution)/shard_map/reshape | solution.py:403
  3.3 46.5 %token_pass.1 = (bf16[8,128,128]{2,1,0:T(8,128)(2,1)}, f32[8,8,128]{2,1,0:T(8,128)}, bf16[8,128,128]{2,1,0:T(8,128)(2,1)}, bf16[8,128,128]{2,1,0:T(8,128)(2,1)},...) custom-call(s32[8,128]{1,0:T(8,128)} %reshape.14.tok_ref, s32[8,128]{1,0:T(8,128)} %reshape.15.lab_ref, ...), custom_call_target="tpu_custom_call" | custom-call | tf_op jit(solution)/shard_map/token_pass/pallas_call | solution.py:411
  49.9 1.3 %slice.11.rank_ref = s32[8,128]{1,0:T(8,128)} slice(s32[16,128]{1,0:T(8,128)} %get-tuple-element.20), slice={[8:16], [0:128]} | slice | bytes 8192 | tf_op jit(solution)/shard_map/slice | solution.py:454
  51.1 1.2 slice_bitcast_fusion.starts_sm
  52.3 64.5 %table_grad.1 = f32[30592,128]{1,0:T(8,128)} custom-call(s32[128]{0:T(128)} %slice_bitcast_fusion.starts_sm, bf16[30592,128]{1,0:T(8,128)(2,1)} %emb_ref.1, bf16[8,128,128]{2,1,0:T(8,128)(2,1)} %get-tuple-element.21.n_ref, f32[8,8,128]{2,1,0:T(8,128)} %get-tuple-element.16.st_ref, s32[8,128]{1,0:T(8,128)} %reshape.15.lab_ref, ...), custom_call_target="tpu_custom_call" | custom-call | tf_op jit(solution)/shard_map/table_grad/pallas_call | solution.py:440
  116.9 4.8 %weight_grads.1 = (f32[128,512]{1,0:T(8,128)}, f32[512,128]{1,0:T(8,128)}, f32[8,128]{1,0:T(8,128)}) custom-call(bf16[8,128,128]{2,1,0:T(8,128)(2,1)} %get-tuple-element.14.x_ref, bf16[8,128,128]{2,1,0:T(8,128)(2,1)} %get-tuple-element.15.g_ref, bf16[128,512]{1,0:T(8,128)(2,1)} %bitcast.8, bf16[512,128]{1,0:T(8,128)(2,1)} %bitcast.10, ...), custom_call_target="tpu_custom_call" | custom-call | tf_op jit(solution)/shard_map/weight_grads/pallas_call | solution.py:429
  121.7 1.2 slice.9

commit v2 on v1

--- a/solution.py
+++ b/solution.py
@@ -15,7 +15,7 @@
 LN2 = math.log(2.0)
 GELU_C = math.sqrt(2.0 / math.pi)
 HEAD_BLOCK = 2048
-EMB_BLOCK = 512
+EMB_BLOCK = 1024
 VMEM_BYTES = 60 * 1024 * 1024
 
 
@@ -45,6 +45,11 @@
     return jnp.transpose(jnp.broadcast_to(row, (size, size)))
 
 
+def joined_row(ref, i, size):
+    per = size // ref.shape[1]
+    return jnp.concatenate([ref[pl.ds(i * per + k, 1), :] for k in range(per)], axis=1)
+
+
 def row_of(col, size):
     eye = lax.broadcasted_iota(jnp.int32, (size, size), 0) == lax.broadcasted_iota(jnp.int32, (size, size), 1)
     return jnp.sum(jnp.where(eye, jnp.broadcast_to(col, (size, size)), 0.0), axis=0, keepdims=True)
@@ -52,7 +57,7 @@
 
 def token_kernel(
     n_stage, tok_ref, lab_ref, emb_hbm, wup_hbm, wdn_hbm,
-    n_out, st_out, xs_out, gs_out, dx_out, ids_out, starts_out,
+    n_out, st_out, xs_out, gs_out, dx_out, ids_out, rank_out, lab_out, starts_out,
     wup, wdn, emb, z_buf, xs, gs, pre, n_loc, st_loc, gat,
     loc_sem, wsend, upr, dnr, xsend, xrecv, gsend, grecv, nsend, nrecv, ssend, srecv, dsend, drecv,
 ):
@@ -96,7 +101,7 @@
     for copy in first:
         copy.start()
 
-    tok_row = tok_ref[...]
+    tok_row = jnp.concatenate([joined_row(tok_ref, i, tok_n) for i in range(n_stage)], axis=0)
     pos = lax.broadcasted_iota(jnp.int32, (n_stage, tok_n), 0) * tok_n + lax.broadcasted_iota(jnp.int32, (n_stage, tok_n), 1)
     key_row = tok_row * total + pos
     lane = lax.broadcasted_iota(jnp.int32, (tok_n, tok_n), 1)
@@ -117,13 +122,14 @@
     acc = jnp.zeros((tok_n, tok_n), jnp.int32)
     for j in range(n_stage):
         acc = acc + jnp.where(tok_cols[j] < lane * EMB_BLOCK, 1, 0)
-    starts_out[0:8, :] = jnp.broadcast_to(jnp.sum(acc, axis=0, keepdims=True), (8, tok_n))
+    starts_out[...] = jnp.sum(acc, axis=0, keepdims=True)
     for i in range(n_stage):
-        starts_out[8 + i:9 + i, :] = rank_rows[i]
+        rank_out[i:i + 1, :] = rank_rows[i]
+        lab_out[i:i + 1, :] = joined_row(lab_ref, i, tok_n)
 
     load_emb.wait()
     pick = jnp.concatenate(
-        [column_of(tok_ref[pl.ds(me, 1), :], tok_n), column_of(lab_ref[pl.ds(me, 1), :], tok_n)], axis=0)
+        [column_of(joined_row(tok_ref, me, tok_n), tok_n), column_of(joined_row(lab_ref, me, tok_n), tok_n)], axis=0)
     lane2 = lax.broadcasted_iota(jnp.int32, (2 * tok_n, tok_n), 1)
 
     def blocks(body):
@@ -334,8 +340,7 @@
     gup_ref[...] = jnp.zeros_like(gup_ref)
     gdn_ref[...] = jnp.zeros_like(gdn_ref)
     lax.fori_loop(0, n_stage // step, body, 0)
-    nll = jnp.sum(st_ref[:, 2, :], keepdims=True) * (1.0 / (n_stage * tok_n))
-    loss_ref[...] = jnp.broadcast_to(nll, loss_ref.shape)
+    loss_ref[0] = jnp.sum(st_ref[:, 2, :]) * (1.0 / (n_stage * tok_n))
 
 
 def table_kernel(starts_sm, emb_ref, n_ref, st_ref, lab_ref, dx_ref, ids_ref, rank_ref, out_ref, n_t, level, d_lab, lab16, dxs):
@@ -381,8 +386,8 @@
         hot = jnp.where(row32 == ids_ref[c, 0:1, :] - base, 1.0, 0.0).astype(BF16)
         return dot_nn(hot, dxs[c])
 
-    first = jnp.minimum(starts_sm[blk] // tok_n, n_chunk - 1)
-    last = (starts_sm[blk + 1] + tok_n - 1) // tok_n
+    first = jnp.minimum(starts_sm[0, blk] // tok_n, n_chunk - 1)
+    last = (starts_sm[0, blk + 1] + tok_n - 1) // tok_n
     out_ref[...] = acc * scale + token_term(first)
 
     def more(c, carry):
@@ -400,21 +405,20 @@
         ffn = w_up.shape[2]
         total = tokens.shape[0] * tokens.shape[1]
         tok_n = total // n_stage
-        tok8 = tokens.reshape(n_stage, tok_n)
-        lab8 = labels.reshape(n_stage, tok_n)
         w_up, w_down = w_up[0], w_down[0]
         vmem = pl.BlockSpec(memory_space=pltpu.VMEM)
         hbm = pl.BlockSpec(memory_space=pl.ANY)
         dma = pltpu.SemaphoreType.DMA
         n_blk = pl.cdiv(vocab, EMB_BLOCK)
         act = jax.ShapeDtypeStruct((n_stage, tok_n, dim), BF16)
-        n_all, st_all, xs_all, gs_all, dx_all, ids, starts = pl.pallas_call(
+        n_all, st_all, xs_all, gs_all, dx_all, ids, rank, lab8, starts = pl.pallas_call(
             functools.partial(token_kernel, n_stage),
             out_shape=[act, jax.ShapeDtypeStruct((n_stage, 8, tok_n), F32), act, act, act,
                        jax.ShapeDtypeStruct((n_stage, 8, tok_n), jnp.int32),
-                       jax.ShapeDtypeStruct((8 + n_stage, tok_n), jnp.int32)],
+                       jax.ShapeDtypeStruct((n_stage, tok_n), jnp.int32), jax.ShapeDtypeStruct((n_stage, tok_n), jnp.int32),
+                       jax.ShapeDtypeStruct((1, tok_n), jnp.int32)],
             in_specs=[vmem, vmem, hbm, hbm, hbm],
-            out_specs=[hbm, hbm, hbm, hbm, hbm, vmem, vmem],
+            out_specs=[hbm] * 5 + [vmem] * 4,
             scratch_shapes=[
                 pltpu.VMEM((n_stage, dim, ffn), BF16), pltpu.VMEM((n_stage, ffn, dim), BF16),
                 pltpu.VMEM((vocab, dim), BF16), pltpu.VMEM((tok_n, vocab), BF16),
@@ -424,13 +428,13 @@
                 dma((5,)), dma((14,))] + [dma((n_stage,))] * 12,
             compiler_params=pltpu.CompilerParams(collective_id=0, has_side_effects=True, vmem_limit_bytes=VMEM_BYTES),
             name="token_pass",
-        )(tok8, lab8, emb_table, w_up, w_down)
+        )(tokens, labels, emb_table, w_up, w_down)
 
         grad_up, grad_down, loss = pl.pallas_call(
             weight_kernel,
             out_shape=[jax.ShapeDtypeStruct((dim, ffn), F32), jax.ShapeDtypeStruct((ffn, dim), F32),
-                       jax.ShapeDtypeStruct((8, 128), F32)],
-            in_specs=[vmem] * 5, out_specs=[vmem] * 3,
+                       jax.ShapeDtypeStruct((1,), F32)],
+            in_specs=[vmem] * 5, out_specs=[vmem, vmem, pl.BlockSpec(memory_space=pltpu.SMEM)],
             compiler_params=pltpu.CompilerParams(vmem_limit_bytes=VMEM_BYTES),
             name="weight_grads",
         )(xs_all, gs_all, w_up, w_down, st_all)
@@ -451,8 +455,8 @@
             out_shape=jax.ShapeDtypeStruct((vocab, dim), F32),
             compiler_params=pltpu.CompilerParams(dimension_semantics=("arbitrary",), vmem_limit_bytes=VMEM_BYTES),
             name="table_grad",
-        )(starts[0], emb_table, n_all, st_all, lab8, dx_all, ids, starts[8:])
-        return loss[0, :1], grad_up[None], grad_down[None], grad_emb
+        )(starts, emb_table, n_all, st_all, lab8, dx_all, ids, rank)
+        return loss, grad_up[None], grad_down[None], grad_emb
 
     return jax.shard_map(
         device_fn, mesh=mesh,

time: 124 us -> 107 us (0.86)
  Pallas kernels: 116 us -> 106 us
  local copies, waits for them, and re-layouts: 6.36 us -> 0 us
    pallas_call x1, Pallas kernels: 64.5 us -> 54.1 us  [device_fn(): pl.pallas_call(table_kernel, grid_spec=pltpu.PrefetchScalarGridSpec(num_s...]
    reshape x2 -> x0, local copies, waits for them, and re-layouts: 2.72 us -> none  [the longest x1 1.36 us: device_fn(): lab8 = labels.reshape(n_stage, tok_n)]
    slice x2 -> x0, local copies, waits for them, and re-layouts: 2.46 us -> none  [the longest x1 1.26 us: device_fn(): starts[8:]]
where the time goes in v2:
time: 107 us; the launch traced here: 106 us
  Pallas kernels  106 us (99%)
    pallas_call x1, Pallas kernels, device_fn(): pl.pallas_call(table_kernel, grid_spec=pltpu.PrefetchScalarGridSpec(num_s...  54.1 us
    pallas_call x1, Pallas kernels, device_fn(): pl.pallas_call(functools.partial(token_kernel, n_stage), out_shape=[act,...  46.7 us
    pallas_call x1, Pallas kernels, device_fn(): pl.pallas_call(weight_kernel, out_shape=[jax.ShapeDtypeStruct((dim, ffn),...  4.87 us

profile of v2, /device:TPU:81, one launch (start us, length us, event | category | flops | bytes accessed | tf_op | source)
XLA Modules:
  0.0 106.4 jit_solution(10334301118964314329)
XLA Ops:
  0.6 46.7 %token_pass.1 = (bf16[8,128,128]{2,1,0:T(8,128)(2,1)}, f32[8,8,128]{2,1,0:T(8,128)}, bf16[8,128,128]{2,1,0:T(8,128)(2,1)}, bf16[8,128,128]{2,1,0:T(8,128)(2,1)},...) custom-call(s32[16,64]{1,0:T(8,128)} %tok_ref.1, ...), custom_call_target="tpu_custom_call" | custom-call | tf_op jit(solution)/shard_map/token_pass/pallas_call | solution.py:414
  47.4 54.1 %table_grad.1 = f32[30592,128]{1,0:T(8,128)} custom-call(s32[1,128]{1,0:T(1,128)} %get-tuple-element.22.starts_sm, bf16[30592,128]{1,0:T(8,128)(2,1)} %emb_ref.1, bf16[8,128,128]{2,1,0:T(8,128)(2,1)} %get-tuple-element.23.n_ref, f32[8,8,128]{2,1,0:T(8,128)} %get-tuple-element.18.st_ref, s32[8,128]{1,0:T(8,128)} %get-tuple-element.24.lab_ref, ...), custom_call_target="tpu_custom_call" | custom-call | tf_op jit(solution)/shard_map/table_grad/pallas_call | solution.py:444
  101.5 4.9 %weight_grads.1 = (f32[128,512]{1,0:T(8,128)}, f32[512,128]{1,0:T(8,128)}, f32[1]{0:T(128)}) custom-call(bf16[8,128,128]{2,1,0:T(8,128)(2,1)} %get-tuple-element.16.x_ref, bf16[8,128,128]{2,1,0:T(8,128)(2,1)} %get-tuple-element.17.g_ref, bf16[128,512]{1,0:T(8,128)(2,1)} %bitcast.5, bf16[512,128]{1,0:T(8,128)(2,1)} %bitcast.7, ...), custom_call_target="tpu_custom_call" | custom-call | tf_op jit(solution)/shard_map/weight_grads/pallas_call | solution.py:433

commit v3 on v2

--- a/solution.py
+++ b/solution.py
@@ -15,7 +15,8 @@
 LN2 = math.log(2.0)
 GELU_C = math.sqrt(2.0 / math.pi)
 HEAD_BLOCK = 2048
-EMB_BLOCK = 1024
+TABLE_BLOCK = 1024
+EMB_BLOCK = 2048
 VMEM_BYTES = 60 * 1024 * 1024
 
 
@@ -57,9 +58,9 @@
 
 def token_kernel(
     n_stage, tok_ref, lab_ref, emb_hbm, wup_hbm, wdn_hbm,
-    n_out, st_out, xs_out, gs_out, dx_out, ids_out, rank_out, lab_out, starts_out,
-    wup, wdn, emb, z_buf, xs, gs, pre, n_loc, st_loc, gat,
-    loc_sem, wsend, upr, dnr, xsend, xrecv, gsend, grecv, nsend, nrecv, ssend, srecv, dsend, drecv,
+    st_out, xs_out, gs_out, dx_out, table_out, ids_out, rank_out, starts_out,
+    wup, wdn, emb, z_buf, xs, gs, pre, n_all, st_all, gat, n_t, level_t, d_lab_t, table,
+    loc_sem, wsend, upr, dnr, xsend, xrecv, gsend, grecv, nsend, nrecv, ssend, srecv, dsend, drecv, tsend, trecv, tloc,
 ):
     me = lax.axis_index("stage")
     n_chip = n_stage // 2
@@ -69,7 +70,7 @@
     left = lax.rem(chip + n_chip - 1, n_chip) * 2 + core
     far = lax.rem(chip + 2, n_chip) * 2 + core
     peers = [lax.rem(me + d, n_stage) for d in range(1, n_stage)]
-    tok_n, dim = n_loc.shape
+    _, tok_n, dim = n_all.shape
     vocab = emb.shape[0]
     total = n_stage * tok_n
     scale = dim ** -0.5
@@ -119,13 +120,13 @@
         for j in range(n_stage):
             acc = acc + jnp.where(rank_cols[j] == lane + c * tok_n, tok_cols[j], 0)
         ids_out[c] = jnp.broadcast_to(jnp.sum(acc, axis=0, keepdims=True), (8, tok_n))
+    ids_out[n_stage] = jnp.full((8, tok_n), -1, jnp.int32)
     acc = jnp.zeros((tok_n, tok_n), jnp.int32)
     for j in range(n_stage):
         acc = acc + jnp.where(tok_cols[j] < lane * EMB_BLOCK, 1, 0)
     starts_out[...] = jnp.sum(acc, axis=0, keepdims=True)
     for i in range(n_stage):
         rank_out[i:i + 1, :] = rank_rows[i]
-        lab_out[i:i + 1, :] = joined_row(lab_ref, i, tok_n)
 
     load_emb.wait()
     pick = jnp.concatenate(
@@ -216,14 +217,14 @@
     x_last = xs[n_stage].astype(F32)
     inv = lax.rsqrt(jnp.mean(x_last * x_last, axis=-1, keepdims=True) + 1e-6)
     n_val = (x_last * inv).astype(BF16)
-    n_loc[...] = n_val
+    n_all[me] = n_val
 
     def spread(src, dst, send, recv):
         return [pltpu.make_async_remote_copy(src, dst.at[me], send.at[d], recv.at[me], device_id={"stage": peer},
                                              device_id_type=MESH) for d, peer in enumerate(peers)]
 
     def stat_block(v0, size):
-        z = (dot_nt(n_loc[...], emb[pl.ds(v0, size), :]) * scale).astype(BF16)
+        z = (dot_nt(n_all[me], emb[pl.ds(v0, size), :]) * scale).astype(BF16)
         z_buf[:, pl.ds(v0, size)] = z
         parts = [z[:, j * tok_n:(j + 1) * tok_n].astype(F32) for j in range(size // tok_n)]
         m_old = gat[0:tok_n, :]
@@ -236,11 +237,9 @@
 
     gat[0:tok_n, :] = jnp.full((tok_n, dim), -1e30, F32)
     gat[tok_n:2 * tok_n, :] = jnp.zeros((tok_n, dim), F32)
-    send_n = spread(n_loc, n_out, nsend, nrecv)
+    send_n = spread(n_all.at[me], n_all, nsend, nrecv)
     for copy in send_n:
         copy.start()
-    own_n = pltpu.make_async_copy(n_loc, n_out.at[me], loc_sem.at[2])
-    own_n.start()
     blocks(stat_block)
     m_lane = gat[0:tok_n, :]
     m_tok = jnp.max(m_lane, axis=-1, keepdims=True)
@@ -253,16 +252,14 @@
     p_lab = jnp.exp2(z_lab * LOG2E - level)
     d_lab = (p_lab - 1.0 / total).astype(BF16).astype(F32)
     p_lab = p_lab.astype(BF16).astype(F32)
-    st_loc[...] = jnp.concatenate(
+    st_all[me] = jnp.concatenate(
         [row_of(level, tok_n), row_of(d_lab, tok_n), row_of(lse - z_lab, tok_n), jnp.zeros((5, tok_n), F32)], axis=0)
     level_full = jnp.broadcast_to(level, (tok_n, tok_n))
 
     gat[0:tok_n, :] = (d_lab - p_lab) * lab_rows
-    send_s = spread(st_loc, st_out, ssend, srecv)
+    send_s = spread(st_all.at[me], st_all, ssend, srecv)
     for copy in send_s:
         copy.start()
-    own_s = pltpu.make_async_copy(st_loc, st_out.at[me], loc_sem.at[3])
-    own_s.start()
 
     def grad_block(v0, size):
         parts = []
@@ -300,22 +297,92 @@
     own_d = pltpu.make_async_copy(gs.at[0], dx_out.at[me], loc_sem.at[4])
     own_d.start()
 
+    for peer in peers:
+        for buf, send, recv in ((n_all, nsend, nrecv), (st_all, ssend, srecv)):
+            pltpu.make_async_remote_copy(buf.at[peer], buf.at[peer], send.at[0], recv.at[peer],
+                                         device_id={"stage": peer}, device_id_type=MESH).wait_recv()
+    own_s = pltpu.make_async_copy(st_all, st_out, loc_sem.at[3])
+    own_s.start()
+    for i in range(n_stage):
+        cols = slice(i * tok_n, (i + 1) * tok_n)
+        n_t[:, cols] = jnp.transpose(n_all[i])
+        level_t[:, cols] = jnp.broadcast_to(st_all[i, 0:1, :], (8, tok_n))
+        d_lab_t[:, cols] = jnp.broadcast_to(st_all[i, 1:2, :], (16, tok_n)).astype(BF16)
+    half = vocab // 2
+    wide = 2 * tok_n
+
+    def table_copies(j, size):
+        local = pl.ds(pl.multiple_of(j * TABLE_BLOCK, 16), size)
+        rows = pl.ds(pl.multiple_of(core * half + j * TABLE_BLOCK, 16), size)
+        return (pltpu.make_async_remote_copy(table.at[local], table_out.at[rows], tsend.at[j], trecv.at[j],
+                                             device_id={"stage": sib}, device_id_type=MESH),
+                pltpu.make_async_copy(table.at[local], table_out.at[rows], tloc.at[j]))
+
+    def table_start(j, size):
+        for copy in table_copies(j, size):
+            copy.start()
+
+    def table_block(j, size):
+        base = pl.multiple_of(core * half + j * TABLE_BLOCK, 16)
+        e = emb[pl.ds(base, size), :]
+        row16 = lax.broadcasted_iota(jnp.int16, (size, wide), 0)
+        acc = jnp.zeros((size, dim), F32)
+        for t in range(total // wide):
+            cols = slice(t * wide, (t + 1) * wide)
+            z = (dot_nn(e, n_t[:, cols]) * scale).astype(BF16).astype(F32)
+            p = jnp.exp2(z * LOG2E - level_t[0:1, cols]).astype(BF16)
+            lab = jnp.concatenate([joined_row(lab_ref, 2 * t, tok_n), joined_row(lab_ref, 2 * t + 1, tok_n)], axis=1) - base
+            lab = jnp.broadcast_to(lab, (16, wide)).astype(jnp.int16)
+            dz = jnp.where(row16 == lab[0:1, :], d_lab_t[0:1, cols], p)
+            acc = acc + dot_nn(dz, jnp.concatenate([n_all[2 * t], n_all[2 * t + 1]], axis=0))
+        table[pl.ds(pl.multiple_of(j * TABLE_BLOCK, 16), size), :] = acc * scale
+
+    full, tail = half // TABLE_BLOCK, half % TABLE_BLOCK
+
+    def table_step(j, carry):
+        @pl.when(j > 0)
+        def _():
+            table_start(j - 1, TABLE_BLOCK)
+
+        table_block(j, TABLE_BLOCK)
+        return carry
+
+    lax.fori_loop(0, full, table_step, 0)
+    table_start(full - 1, TABLE_BLOCK)
+    if tail:
+        table_block(full, tail)
+
     for copy in first + second + send_n + send_s:
         copy.wait_send()
-    for copy in (own_x, own_g, own_n, own_s, own_d):
+    for copy in (own_x, own_g, own_s, own_d):
         copy.wait()
-    for d, peer in enumerate(peers):
+    for peer in peers:
         pltpu.make_async_remote_copy(xs.at[peer], xs_out.at[peer], xsend.at[peer], xrecv.at[peer],
                                      device_id={"stage": peer}, device_id_type=MESH).wait()
         pltpu.make_async_remote_copy(gs.at[peer + 1], gs_out.at[peer], gsend.at[peer], grecv.at[peer],
                                      device_id={"stage": peer}, device_id_type=MESH).wait()
-        for src, dst, send, recv in ((n_loc, n_out, nsend, nrecv), (st_loc, st_out, ssend, srecv)):
-            pltpu.make_async_remote_copy(src, dst.at[peer], send.at[d], recv.at[peer],
-                                         device_id={"stage": peer}, device_id_type=MESH).wait_recv()
-        pltpu.make_async_remote_copy(gs.at[0], dx_out.at[peer], dsend.at[d], drecv.at[peer],
+        pltpu.make_async_remote_copy(gs.at[0], dx_out.at[peer], dsend.at[0], drecv.at[peer],
                                      device_id={"stage": peer}, device_id_type=MESH).wait_recv()
     for copy in send_d:
         copy.wait_send()
+    if tail:
+        table_start(full, tail)
+
+    def table_wait(j, size):
+        remote, local = table_copies(j, size)
+        remote.wait_send()
+        local.wait()
+        rows = pl.ds(pl.multiple_of((1 - core) * half + j * TABLE_BLOCK, 16), size)
+        pltpu.make_async_remote_copy(table.at[pl.ds(pl.multiple_of(j * TABLE_BLOCK, 16), size)], table_out.at[rows],
+                                     tsend.at[j], trecv.at[j], device_id={"stage": sib}, device_id_type=MESH).wait_recv()
+
+    def wait_step(j, carry):
+        table_wait(j, TABLE_BLOCK)
+        return carry
+
+    lax.fori_loop(0, full, wait_step, 0)
+    if tail:
+        table_wait(full, tail)
 
 
 def weight_kernel(x_ref, g_ref, wup_ref, wdn_ref, st_ref, gup_ref, gdn_ref, loss_ref):
@@ -343,58 +410,39 @@
     loss_ref[0] = jnp.sum(st_ref[:, 2, :]) * (1.0 / (n_stage * tok_n))
 
 
-def table_kernel(starts_sm, emb_ref, n_ref, st_ref, lab_ref, dx_ref, ids_ref, rank_ref, out_ref, n_t, level, d_lab, lab16, dxs):
-    n_chunk, tok_n, dim = n_ref.shape
-    total = n_chunk * tok_n
+def table_kernel(starts_sm, part_ref, dx_ref, ids_ref, rank_ref, out_ref, dxs):
+    n_chunk, tok_n, dim = dx_ref.shape
     blk = pl.program_id(0)
     rows = out_ref.shape[0]
-    scale = dim ** -0.5
 
     @pl.when(blk == 0)
     def _():
         row_id = lax.broadcasted_iota(jnp.int32, (tok_n, tok_n), 0)
-        for i in range(n_chunk):
-            cols = slice(i * tok_n, (i + 1) * tok_n)
-            n_t[:, cols] = jnp.transpose(n_ref[i])
-            level[:, cols] = jnp.broadcast_to(st_ref[i, 0:1, :], (8, tok_n))
-            d_lab[:, cols] = jnp.broadcast_to(st_ref[i, 1:2, :], (16, tok_n)).astype(BF16)
         for c in range(n_chunk):
             acc = jnp.zeros((tok_n, dim), F32)
             for i in range(n_chunk):
                 hot = jnp.where(rank_ref[i:i + 1, :] == row_id + c * tok_n, 1.0, 0.0).astype(BF16)
                 acc = acc + dot_nn(hot, dx_ref[i])
             dxs[c] = acc.astype(BF16)
-
-    wide = 2 * tok_n
-    e = emb_ref[...]
+        dxs[n_chunk] = jnp.zeros((tok_n, dim), BF16)
+
     base = blk * rows
-    acc = jnp.zeros((rows, dim), F32)
-    row16 = lax.broadcasted_iota(jnp.int16, (rows, wide), 0)
-    for t in range(total // wide):
-        cols = slice(t * wide, (t + 1) * wide)
-        z = (dot_nn(e, n_t[:, cols]) * scale).astype(BF16).astype(F32)
-        p = jnp.exp2(z * LOG2E - level[0:1, cols]).astype(BF16)
-        lab = jnp.concatenate([lab_ref[2 * t:2 * t + 1, :], lab_ref[2 * t + 1:2 * t + 2, :]], axis=1) - base
-        lab = jnp.broadcast_to(lab, (16, wide)).astype(jnp.int16)
-        dz = jnp.where(row16 == lab[0:1, :], d_lab[0:1, cols], p)
-        nn = jnp.concatenate([n_ref[2 * t], n_ref[2 * t + 1]], axis=0)
-        acc = acc + dot_nn(dz, nn)
-
-    row32 = lax.broadcasted_iota(jnp.int32, (rows, tok_n), 0)
-
-    def token_term(c):
-        hot = jnp.where(row32 == ids_ref[c, 0:1, :] - base, 1.0, 0.0).astype(BF16)
-        return dot_nn(hot, dxs[c])
+    row16 = lax.broadcasted_iota(jnp.int16, (rows, tok_n), 0)
+
+    def hot_rows(c):
+        ids = jnp.broadcast_to(ids_ref[c, 0:1, :] - base, (16, tok_n)).astype(jnp.int16)
+        return jnp.where(row16 == ids[0:1, :], jnp.ones((), BF16), jnp.zeros((), BF16))
 
     first = jnp.minimum(starts_sm[0, blk] // tok_n, n_chunk - 1)
     last = (starts_sm[0, blk + 1] + tok_n - 1) // tok_n
-    out_ref[...] = acc * scale + token_term(first)
+    out_ref[...] = part_ref[...] + dot_nn(jnp.concatenate([hot_rows(first), hot_rows(first + 1)], axis=1),
+                                          jnp.concatenate([dxs[first], dxs[first + 1]], axis=0))
 
     def more(c, carry):
-        out_ref[...] += token_term(c)
+        out_ref[...] += dot_nn(hot_rows(c), dxs[c])
         return carry
 
-    lax.fori_loop(first + 1, last, more, 0)
+    lax.fori_loop(first + 2, last, more, 0)
 
 
 def solution(mesh):
@@ -411,21 +459,23 @@
         dma = pltpu.SemaphoreType.DMA
         n_blk = pl.cdiv(vocab, EMB_BLOCK)
         act = jax.ShapeDtypeStruct((n_stage, tok_n, dim), BF16)
-        n_all, st_all, xs_all, gs_all, dx_all, ids, rank, lab8, starts = pl.pallas_call(
+        st_all, xs_all, gs_all, dx_all, part, ids, rank, starts = pl.pallas_call(
             functools.partial(token_kernel, n_stage),
-            out_shape=[act, jax.ShapeDtypeStruct((n_stage, 8, tok_n), F32), act, act, act,
-                       jax.ShapeDtypeStruct((n_stage, 8, tok_n), jnp.int32),
-                       jax.ShapeDtypeStruct((n_stage, tok_n), jnp.int32), jax.ShapeDtypeStruct((n_stage, tok_n), jnp.int32),
-                       jax.ShapeDtypeStruct((1, tok_n), jnp.int32)],
+            out_shape=[jax.ShapeDtypeStruct((n_stage, 8, tok_n), F32), act, act, act,
+                       jax.ShapeDtypeStruct((vocab, dim), F32),
+                       jax.ShapeDtypeStruct((n_stage + 1, 8, tok_n), jnp.int32),
+                       jax.ShapeDtypeStruct((n_stage, tok_n), jnp.int32), jax.ShapeDtypeStruct((1, tok_n), jnp.int32)],
             in_specs=[vmem, vmem, hbm, hbm, hbm],
-            out_specs=[hbm] * 5 + [vmem] * 4,
+            out_specs=[hbm] * 5 + [vmem] * 3,
             scratch_shapes=[
                 pltpu.VMEM((n_stage, dim, ffn), BF16), pltpu.VMEM((n_stage, ffn, dim), BF16),
                 pltpu.VMEM((vocab, dim), BF16), pltpu.VMEM((tok_n, vocab), BF16),
                 pltpu.VMEM((n_stage + 1, tok_n, dim), BF16), pltpu.VMEM((n_stage + 1, tok_n, dim), BF16),
-                pltpu.VMEM((n_stage, tok_n, ffn), BF16), pltpu.VMEM((tok_n, dim), BF16),
-                pltpu.VMEM((8, tok_n), F32), pltpu.VMEM((2 * tok_n, dim), F32),
-                dma((5,)), dma((14,))] + [dma((n_stage,))] * 12,
+                pltpu.VMEM((n_stage, tok_n, ffn), BF16), pltpu.VMEM((n_stage, tok_n, dim), BF16),
+                pltpu.VMEM((n_stage, 8, tok_n), F32), pltpu.VMEM((2 * tok_n, dim), F32),
+                pltpu.VMEM((dim, total), BF16), pltpu.VMEM((8, total), F32), pltpu.VMEM((16, total), BF16),
+                pltpu.VMEM((vocab // 2, dim), F32),
+                dma((5,)), dma((14,))] + [dma((n_stage,))] * 12 + [dma((pl.cdiv(vocab // 2, TABLE_BLOCK),))] * 3,
             compiler_params=pltpu.CompilerParams(collective_id=0, has_side_effects=True, vmem_limit_bytes=VMEM_BYTES),
             name="token_pass",
         )(tokens, labels, emb_table, w_up, w_down)
@@ -445,17 +495,14 @@
             table_kernel,
             grid_spec=pltpu.PrefetchScalarGridSpec(
                 num_scalar_prefetch=1, grid=(n_blk,),
-                in_specs=[pl.BlockSpec((EMB_BLOCK, dim), lambda i, s: (i, 0)),
-                          pl.BlockSpec((n_stage, tok_n, dim), whole3), pl.BlockSpec((n_stage, 8, tok_n), whole3),
-                          pl.BlockSpec((n_stage, tok_n), whole2), pl.BlockSpec((n_stage, tok_n, dim), whole3),
-                          pl.BlockSpec((n_stage, 8, tok_n), whole3), pl.BlockSpec((n_stage, tok_n), whole2)],
+                in_specs=[pl.BlockSpec((EMB_BLOCK, dim), lambda i, s: (i, 0)), pl.BlockSpec((n_stage, tok_n, dim), whole3),
+                          pl.BlockSpec((n_stage + 1, 8, tok_n), whole3), pl.BlockSpec((n_stage, tok_n), whole2)],
                 out_specs=pl.BlockSpec((EMB_BLOCK, dim), lambda i, s: (i, 0)),
-                scratch_shapes=[pltpu.VMEM((dim, total), BF16), pltpu.VMEM((8, total), F32), pltpu.VMEM((16, total), BF16),
-                                pltpu.VMEM((16, total), jnp.int16), pltpu.VMEM((n_stage, tok_n, dim), BF16)]),
+                scratch_shapes=[pltpu.VMEM((n_stage + 1, tok_n, dim), BF16)]),
             out_shape=jax.ShapeDtypeStruct((vocab, dim), F32),
             compiler_params=pltpu.CompilerParams(dimension_semantics=("arbitrary",), vmem_limit_bytes=VMEM_BYTES),
             name="table_grad",
-        )(starts, emb_table, n_all, st_all, lab8, dx_all, ids, rank)
+        )(starts, part, dx_all, ids, rank)
         return loss, grad_up[None], grad_down[None], grad_emb
 
     return jax.shard_map(

time: 107 us -> 93.3 us (0.87)
  Pallas kernels: 106 us -> 92.1 us
    pallas_call x1, Pallas kernels: 54.1 us -> 22.3 us  [device_fn(): pl.pallas_call(table_kernel, grid_spec=pltpu.PrefetchScalarGridSpec(num_s...]
    pallas_call x1, Pallas kernels: 46.7 us -> 64.9 us  [device_fn(): pl.pallas_call(functools.partial(token_kernel, n_stage), out_shape=[jax.S...]
where the time goes in v3:
time: 93.3 us; the launch traced here: 92.8 us
  Pallas kernels  92.1 us (99%)
    pallas_call x1, Pallas kernels, device_fn(): pl.pallas_call(functools.partial(token_kernel, n_stage), out_shape=[jax.S...  64.9 us
    pallas_call x1, Pallas kernels, device_fn(): pl.pallas_call(table_kernel, grid_spec=pltpu.PrefetchScalarGridSpec(num_s...  22.3 us
    pallas_call x1, Pallas kernels, device_fn(): pl.pallas_call(weight_kernel, out_shape=[jax.ShapeDtypeStruct((dim, ffn),...  4.86 us

profile of v3, /device:TPU:81, one launch (start us, length us, event | category | flops | bytes accessed | tf_op | source)
XLA Modules:
  0.0 92.8 jit_solution(15515566161010786950)
XLA Ops:
  0.6 64.9 %token_pass.1 = (f32[8,8,128]{2,1,0:T(8,128)}, bf16[8,128,128]{2,1,0:T(8,128)(2,1)}, bf16[8,128,128]{2,1,0:T(8,128)(2,1)}, bf16[8,128,128]{2,1,0:T(8,128)(2,1)},...) custom-call(s32[16,64]{1,0:T(8,128)} %tok_ref.1, s32[16,64]{1,0:T(8,128)} %lab_ref.1, ...), custom_call_target="tpu_custom_call" | custom-call | tf_op jit(solution)/shard_map/token_pass/pallas_call | solution.py:462
  65.6 4.9 %weight_grads.1 = (f32[128,512]{1,0:T(8,128)}, f32[512,128]{1,0:T(8,128)}, f32[1]{0:T(128)}) custom-call(bf16[8,128,128]{2,1,0:T(8,128)(2,1)} %get-tuple-element.15.x_ref, bf16[8,128,128]{2,1,0:T(8,128)(2,1)} %get-tuple-element.16.g_ref, bf16[128,512]{1,0:T(8,128)(2,1)} %bitcast.5, bf16[512,128]{1,0:T(8,128)(2,1)} %bitcast.7, ...), custom_call_target="tpu_custom_call" | custom-call | tf_op jit(solution)/shard_map/weight_grads/pallas_call | solution.py:483
  70.4 22.3 %table_grad.1 = f32[30592,128]{1,0:T(8,128)} custom-call(s32[1,128]{1,0:T(1,128)} %get-tuple-element.21.starts_sm, f32[30592,128]{1,0:T(8,128)} %get-tuple-element.22.part_ref, bf16[8,128,128]{2,1,0:T(8,128)(2,1)} %get-tuple-element.23.dx_ref, s32[9,8,128]{2,1,0:T(8,128)} %get-tuple-element.24.ids_ref, s32[8,128]{1,0:T(8,128)} %get-tuple-element.25.rank_ref), custom_call_target="tpu_custom_call" | custom-call | tf_op jit(solution)/shard_map/table_grad/pallas_call | solution.py:494

commit v4 on v3

--- a/solution.py
+++ b/solution.py
@@ -16,7 +16,7 @@
 GELU_C = math.sqrt(2.0 / math.pi)
 HEAD_BLOCK = 2048
 TABLE_BLOCK = 1024
-EMB_BLOCK = 2048
+EMB_BLOCK = 1024
 VMEM_BYTES = 60 * 1024 * 1024
 
 
@@ -385,64 +385,89 @@
         table_wait(full, tail)
 
 
-def weight_kernel(x_ref, g_ref, wup_ref, wdn_ref, st_ref, gup_ref, gdn_ref, loss_ref):
-    n_stage, tok_n, _ = x_ref.shape
-    step = 2
-
-    def body(i, carry):
-        x = jnp.concatenate([x_ref[step * i + k] for k in range(step)], axis=0)
-        g = jnp.concatenate([g_ref[step * i + k] for k in range(step)], axis=0)
+def finish_kernel(
+    starts_sm, part_hbm, x_ref, g_ref, wup_ref, wdn_ref, st_ref, dx_ref, ids_ref, rank_ref,
+    out_hbm, gup_hbm, gdn_hbm, loss_ref,
+    buf, dxs, hid, da, gup, gdn, read_sem, write_sem, grad_sem,
+):
+    n_chunk, tok_n, dim = dx_ref.shape
+    vocab = buf.shape[0]
+    ffn = hid.shape[1]
+    full, tail = vocab // EMB_BLOCK, vocab % EMB_BLOCK
+
+    def span(j, size):
+        return pl.ds(pl.multiple_of(j * EMB_BLOCK, 16), size)
+
+    def read(j, size):
+        return pltpu.make_async_copy(part_hbm.at[span(j, size)], buf.at[span(j, size)], read_sem.at[j])
+
+    def write(j, size):
+        return pltpu.make_async_copy(buf.at[span(j, size)], out_hbm.at[span(j, size)], write_sem.at[j])
+
+    def each(fn):
+        def step(j, carry):
+            fn(j, EMB_BLOCK)
+            return carry
+
+        lax.fori_loop(0, full, step, 0)
+        if tail:
+            fn(full, tail)
+
+    each(lambda j, size: read(j, size).start())
+
+    step_n = 2 * tok_n
+    for i in range(n_chunk // 2):
+        x = jnp.concatenate([x_ref[2 * i], x_ref[2 * i + 1]], axis=0)
+        g = jnp.concatenate([g_ref[2 * i], g_ref[2 * i + 1]], axis=0)
         a = dot_nn(x, wup_ref[...]).astype(BF16).astype(F32)
         sq = a * a
         t = jnp.tanh(GELU_C * (a + 0.044715 * (sq * a)))
         cdf = 0.5 * (1.0 + t)
-        h = (a * cdf).astype(BF16)
+        hid[i * step_n:(i + 1) * step_n, :] = (a * cdf).astype(BF16)
         slope = cdf + (0.5 * a) * (1.0 - t * t) * (GELU_C * (1.0 + (3.0 * 0.044715) * sq))
         dh = dot_nt(g, wdn_ref[...]).astype(BF16).astype(F32)
-        da = (dh * slope).astype(BF16)
-        gup_ref[...] += dot_tn(x, da)
-        gdn_ref[...] += dot_tn(h, g)
-        return carry
-
-    gup_ref[...] = jnp.zeros_like(gup_ref)
-    gdn_ref[...] = jnp.zeros_like(gdn_ref)
-    lax.fori_loop(0, n_stage // step, body, 0)
-    loss_ref[0] = jnp.sum(st_ref[:, 2, :]) * (1.0 / (n_stage * tok_n))
-
-
-def table_kernel(starts_sm, part_ref, dx_ref, ids_ref, rank_ref, out_ref, dxs):
-    n_chunk, tok_n, dim = dx_ref.shape
-    blk = pl.program_id(0)
-    rows = out_ref.shape[0]
-
-    @pl.when(blk == 0)
-    def _():
-        row_id = lax.broadcasted_iota(jnp.int32, (tok_n, tok_n), 0)
-        for c in range(n_chunk):
-            acc = jnp.zeros((tok_n, dim), F32)
-            for i in range(n_chunk):
-                hot = jnp.where(rank_ref[i:i + 1, :] == row_id + c * tok_n, 1.0, 0.0).astype(BF16)
-                acc = acc + dot_nn(hot, dx_ref[i])
-            dxs[c] = acc.astype(BF16)
-        dxs[n_chunk] = jnp.zeros((tok_n, dim), BF16)
-
-    base = blk * rows
-    row16 = lax.broadcasted_iota(jnp.int16, (rows, tok_n), 0)
-
-    def hot_rows(c):
-        ids = jnp.broadcast_to(ids_ref[c, 0:1, :] - base, (16, tok_n)).astype(jnp.int16)
-        return jnp.where(row16 == ids[0:1, :], jnp.ones((), BF16), jnp.zeros((), BF16))
-
-    first = jnp.minimum(starts_sm[0, blk] // tok_n, n_chunk - 1)
-    last = (starts_sm[0, blk + 1] + tok_n - 1) // tok_n
-    out_ref[...] = part_ref[...] + dot_nn(jnp.concatenate([hot_rows(first), hot_rows(first + 1)], axis=1),
-                                          jnp.concatenate([dxs[first], dxs[first + 1]], axis=0))
-
-    def more(c, carry):
-        out_ref[...] += dot_nn(hot_rows(c), dxs[c])
-        return carry
-
-    lax.fori_loop(first + 2, last, more, 0)
+        da[i * step_n:(i + 1) * step_n, :] = (dh * slope).astype(BF16)
+    gup[...] = dot_tn(x_ref[...].reshape(n_chunk * tok_n, dim), da[...])
+    gdn[...] = jnp.transpose(dot_tn(g_ref[...].reshape(n_chunk * tok_n, dim), hid[...]))
+    grads = [pltpu.make_async_copy(gup, gup_hbm, grad_sem.at[0]), pltpu.make_async_copy(gdn, gdn_hbm, grad_sem.at[1])]
+    for copy in grads:
+        copy.start()
+    loss_ref[0] = jnp.sum(st_ref[:, 2, :]) * (1.0 / (n_chunk * tok_n))
+
+    row_id = lax.broadcasted_iota(jnp.int32, (tok_n, tok_n), 0)
+    for c in range(n_chunk):
+        acc = jnp.zeros((tok_n, dim), F32)
+        for i in range(n_chunk):
+            hot = jnp.where(rank_ref[i:i + 1, :] == row_id + c * tok_n, 1.0, 0.0).astype(BF16)
+            acc = acc + dot_nn(hot, dx_ref[i])
+        dxs[c] = acc.astype(BF16)
+    dxs[n_chunk] = jnp.zeros((tok_n, dim), BF16)
+
+    def add_tokens(j, size):
+        read(j, size).wait()
+        rows = span(j, size)
+        row16 = lax.broadcasted_iota(jnp.int16, (size, tok_n), 0)
+
+        def hot_rows(c):
+            ids = jnp.broadcast_to(ids_ref[c, 0:1, :] - j * EMB_BLOCK, (16, tok_n)).astype(jnp.int16)
+            return jnp.where(row16 == ids[0:1, :], jnp.ones((), BF16), jnp.zeros((), BF16))
+
+        first = jnp.minimum(starts_sm[0, j] // tok_n, n_chunk - 1)
+        last = (starts_sm[0, j + 1] + tok_n - 1) // tok_n
+        buf[rows, :] += dot_nn(jnp.concatenate([hot_rows(first), hot_rows(first + 1)], axis=1),
+                               jnp.concatenate([dxs[first], dxs[first + 1]], axis=0))
+
+        def more(c, carry):
+            buf[rows, :] += dot_nn(hot_rows(c), dxs[c])
+            return carry
+
+        lax.fori_loop(first + 2, last, more, 0)
+        write(j, size).start()
+
+    each(add_tokens)
+    each(lambda j, size: write(j, size).wait())
+    for copy in grads:
+        copy.wait()
 
 
 def solution(mesh):
@@ -457,7 +482,6 @@
         vmem = pl.BlockSpec(memory_space=pltpu.VMEM)
         hbm = pl.BlockSpec(memory_space=pl.ANY)
         dma = pltpu.SemaphoreType.DMA
-        n_blk = pl.cdiv(vocab, EMB_BLOCK)
         act = jax.ShapeDtypeStruct((n_stage, tok_n, dim), BF16)
         st_all, xs_all, gs_all, dx_all, part, ids, rank, starts = pl.pallas_call(
             functools.partial(token_kernel, n_stage),
@@ -480,29 +504,20 @@
             name="token_pass",
         )(tokens, labels, emb_table, w_up, w_down)
 
-        grad_up, grad_down, loss = pl.pallas_call(
-            weight_kernel,
-            out_shape=[jax.ShapeDtypeStruct((dim, ffn), F32), jax.ShapeDtypeStruct((ffn, dim), F32),
-                       jax.ShapeDtypeStruct((1,), F32)],
-            in_specs=[vmem] * 5, out_specs=[vmem, vmem, pl.BlockSpec(memory_space=pltpu.SMEM)],
+        smem = pl.BlockSpec(memory_space=pltpu.SMEM)
+        n_blk = pl.cdiv(vocab, EMB_BLOCK)
+        grad_emb, grad_up, grad_down, loss = pl.pallas_call(
+            finish_kernel,
+            out_shape=[jax.ShapeDtypeStruct((vocab, dim), F32), jax.ShapeDtypeStruct((dim, ffn), F32),
+                       jax.ShapeDtypeStruct((ffn, dim), F32), jax.ShapeDtypeStruct((1,), F32)],
+            in_specs=[smem, hbm] + [vmem] * 8, out_specs=[hbm, hbm, hbm, smem],
+            scratch_shapes=[
+                pltpu.VMEM((vocab, dim), F32), pltpu.VMEM((n_stage + 1, tok_n, dim), BF16),
+                pltpu.VMEM((total, ffn), BF16), pltpu.VMEM((total, ffn), BF16),
+                pltpu.VMEM((dim, ffn), F32), pltpu.VMEM((ffn, dim), F32), dma((n_blk,)), dma((n_blk,)), dma((2,))],
             compiler_params=pltpu.CompilerParams(vmem_limit_bytes=VMEM_BYTES),
-            name="weight_grads",
-        )(xs_all, gs_all, w_up, w_down, st_all)
-
-        whole3 = lambda i, s: (0, 0, 0)
-        whole2 = lambda i, s: (0, 0)
-        grad_emb = pl.pallas_call(
-            table_kernel,
-            grid_spec=pltpu.PrefetchScalarGridSpec(
-                num_scalar_prefetch=1, grid=(n_blk,),
-                in_specs=[pl.BlockSpec((EMB_BLOCK, dim), lambda i, s: (i, 0)), pl.BlockSpec((n_stage, tok_n, dim), whole3),
-                          pl.BlockSpec((n_stage + 1, 8, tok_n), whole3), pl.BlockSpec((n_stage, tok_n), whole2)],
-                out_specs=pl.BlockSpec((EMB_BLOCK, dim), lambda i, s: (i, 0)),
-                scratch_shapes=[pltpu.VMEM((n_stage + 1, tok_n, dim), BF16)]),
-            out_shape=jax.ShapeDtypeStruct((vocab, dim), F32),
-            compiler_params=pltpu.CompilerParams(dimension_semantics=("arbitrary",), vmem_limit_bytes=VMEM_BYTES),
-            name="table_grad",
-        )(starts, part, dx_all, ids, rank)
+            name="finish",
+        )(starts, part, xs_all, gs_all, w_up, w_down, st_all, dx_all, ids, rank)
         return loss, grad_up[None], grad_down[None], grad_emb
 
     return jax.shard_map(

time: 93.3 us -> 81.6 us (0.87)
  Pallas kernels: 92.1 us -> 80.8 us
    pallas_call x2 -> x1, Pallas kernels: 27.2 us -> 15.9 us  [device_fn(): pl.pallas_call(finish_kernel, out_shape=[jax.ShapeDtypeStruct((vocab, dim...]
where the time goes in v4:
time: 81.6 us; the launch traced here: 81.4 us
  Pallas kernels  80.8 us (99%)
    pallas_call x1, Pallas kernels, device_fn(): pl.pallas_call(functools.partial(token_kernel, n_stage), out_shape=[jax.S...  64.9 us
    pallas_call x1, Pallas kernels, device_fn(): pl.pallas_call(finish_kernel, out_shape=[jax.ShapeDtypeStruct((vocab, dim...  15.9 us

profile of v4, /device:TPU:81, one launch (start us, length us, event | category | flops | bytes accessed | tf_op | source)
XLA Modules:
  0.0 81.4 jit_solution(6914031230453249414)
XLA Ops:
  0.6 64.9 %token_pass.1 = (f32[8,8,128]{2,1,0:T(8,128)}, bf16[8,128,128]{2,1,0:T(8,128)(2,1)}, bf16[8,128,128]{2,1,0:T(8,128)(2,1)}, bf16[8,128,128]{2,1,0:T(8,128)(2,1)},...) custom-call(s32[16,64]{1,0:T(8,128)} %tok_ref.1, s32[16,64]{1,0:T(8,128)} %lab_ref.1, ...), custom_call_target="tpu_custom_call" | custom-call | tf_op jit(solution)/shard_map/token_pass/pallas_call | solution.py:486
  65.6 15.9 %finish.1 = (f32[30592,128]{1,0:T(8,128)}, f32[128,512]{1,0:T(8,128)}, f32[512,128]{1,0:T(8,128)}, f32[1]{0:T(128)}) custom-call(s32[1,128]{1,0:T(1,128)} %get-tuple-element.16.starts_sm, f32[30592,128]{1,0:T(8,128)} %get-tuple-element.17.part_hbm, bf16[8,128,128]{2,1,0:T(8,128)(2,1)} %get-tuple-element.18.x_ref, ...), custom_call_target="tpu_custom_call" | custom-call | tf_op jit(solution)/shard_map/finish/pallas_call | solution.py:509

commit v5 on v4

--- a/solution.py
+++ b/solution.py
@@ -14,9 +14,9 @@
 LOG2E = math.log2(math.e)
 LN2 = math.log(2.0)
 GELU_C = math.sqrt(2.0 / math.pi)
-HEAD_BLOCK = 2048
-TABLE_BLOCK = 1024
-EMB_BLOCK = 1024
+HEAD_BLOCK = 4096
+TABLE_BLOCK = 2048
+EMB_BLOCK = 2048
 VMEM_BYTES = 60 * 1024 * 1024
 
 
@@ -57,8 +57,9 @@
 
 
 def token_kernel(
-    n_stage, tok_ref, lab_ref, emb_hbm, wup_hbm, wdn_hbm,
-    st_out, xs_out, gs_out, dx_out, table_out, ids_out, rank_out, starts_out,
+    n_stage, tok_hbm, lab_hbm, emb_hbm, wup_hbm, wdn_hbm,
+    st_out, xs_out, gs_out, dx_out, table_out, ids_hbm, rank_hbm, starts_hbm,
+    tok_ref, lab_ref, ids_out, rank_out, starts_out,
     wup, wdn, emb, z_buf, xs, gs, pre, n_all, st_all, gat, n_t, level_t, d_lab_t, table,
     loc_sem, wsend, upr, dnr, xsend, xrecv, gsend, grecv, nsend, nrecv, ssend, srecv, dsend, drecv, tsend, trecv, tloc,
 ):
@@ -78,14 +79,15 @@
     load_up = pltpu.make_async_copy(wup_hbm, wup.at[me], loc_sem.at[0])
     load_dn = pltpu.make_async_copy(wdn_hbm, wdn.at[me], loc_sem.at[1])
     load_emb = pltpu.make_async_copy(emb_hbm, emb, loc_sem.at[2])
-    load_up.start()
-    load_dn.start()
-    load_emb.start()
+    load_tok = pltpu.make_async_copy(tok_hbm, tok_ref, loc_sem.at[3])
+    load_lab = pltpu.make_async_copy(lab_hbm, lab_ref, loc_sem.at[4])
+    for copy in (load_up, load_dn, load_tok, load_lab, load_emb):
+        copy.start()
 
     barrier = pltpu.get_barrier_semaphore()
-    for peer in peers:
+    for peer in (right, left, sib):
         pl.semaphore_signal(barrier, inc=1, device_id={"stage": peer}, device_id_type=MESH)
-    pl.semaphore_wait(barrier, n_stage - 1)
+    pl.semaphore_wait(barrier, 3)
     load_up.wait()
     load_dn.wait()
 
@@ -102,6 +104,8 @@
     for copy in first:
         copy.start()
 
+    load_tok.wait()
+    load_lab.wait()
     tok_row = jnp.concatenate([joined_row(tok_ref, i, tok_n) for i in range(n_stage)], axis=0)
     pos = lax.broadcasted_iota(jnp.int32, (n_stage, tok_n), 0) * tok_n + lax.broadcasted_iota(jnp.int32, (n_stage, tok_n), 1)
     key_row = tok_row * total + pos
@@ -127,8 +131,12 @@
     starts_out[...] = jnp.sum(acc, axis=0, keepdims=True)
     for i in range(n_stage):
         rank_out[i:i + 1, :] = rank_rows[i]
+    own_i = [pltpu.make_async_copy(ids_out, ids_hbm, loc_sem.at[5]), pltpu.make_async_copy(rank_out, rank_hbm, loc_sem.at[6]),
+             pltpu.make_async_copy(starts_out, starts_hbm, loc_sem.at[7])]
 
     load_emb.wait()
+    for copy in own_i:
+        copy.start()
     pick = jnp.concatenate(
         [column_of(joined_row(tok_ref, me, tok_n), tok_n), column_of(joined_row(lab_ref, me, tok_n), tok_n)], axis=0)
     lane2 = lax.broadcasted_iota(jnp.int32, (2 * tok_n, tok_n), 1)
@@ -354,7 +362,7 @@
 
     for copy in first + second + send_n + send_s:
         copy.wait_send()
-    for copy in (own_x, own_g, own_s, own_d):
+    for copy in (own_x, own_g, own_s, own_d, *own_i):
         copy.wait()
     for peer in peers:
         pltpu.make_async_remote_copy(xs.at[peer], xs_out.at[peer], xsend.at[peer], xrecv.at[peer],
@@ -386,9 +394,10 @@
 
 
 def finish_kernel(
-    starts_sm, part_hbm, x_ref, g_ref, wup_ref, wdn_ref, st_ref, dx_ref, ids_ref, rank_ref,
+    starts_sm, part_hbm, x_hbm, g_hbm, wup_hbm, wdn_hbm, st_hbm, dx_hbm, ids_hbm, rank_hbm,
     out_hbm, gup_hbm, gdn_hbm, loss_ref,
-    buf, dxs, hid, da, gup, gdn, read_sem, write_sem, grad_sem,
+    x_ref, g_ref, wup_ref, wdn_ref, st_ref, dx_ref, ids_ref, rank_ref,
+    buf, dxs, hid, da, gup, gdn, read_sem, write_sem, grad_sem, load_sem,
 ):
     n_chunk, tok_n, dim = dx_ref.shape
     vocab = buf.shape[0]
@@ -413,7 +422,14 @@
         if tail:
             fn(full, tail)
 
+    loads = [pltpu.make_async_copy(src, dst, load_sem.at[i]) for i, (src, dst) in enumerate((
+        (x_hbm, x_ref), (wup_hbm, wup_ref), (g_hbm, g_ref), (wdn_hbm, wdn_ref), (st_hbm, st_ref), (dx_hbm, dx_ref),
+        (ids_hbm, ids_ref), (rank_hbm, rank_ref)))]
+    for copy in loads:
+        copy.start()
     each(lambda j, size: read(j, size).start())
+    for copy in loads:
+        copy.wait()
 
     step_n = 2 * tok_n
     for i in range(n_chunk // 2):
@@ -479,7 +495,6 @@
         total = tokens.shape[0] * tokens.shape[1]
         tok_n = total // n_stage
         w_up, w_down = w_up[0], w_down[0]
-        vmem = pl.BlockSpec(memory_space=pltpu.VMEM)
         hbm = pl.BlockSpec(memory_space=pl.ANY)
         dma = pltpu.SemaphoreType.DMA
         act = jax.ShapeDtypeStruct((n_stage, tok_n, dim), BF16)
@@ -489,9 +504,12 @@
                        jax.ShapeDtypeStruct((vocab, dim), F32),
                        jax.ShapeDtypeStruct((n_stage + 1, 8, tok_n), jnp.int32),
                        jax.ShapeDtypeStruct((n_stage, tok_n), jnp.int32), jax.ShapeDtypeStruct((1, tok_n), jnp.int32)],
-            in_specs=[vmem, vmem, hbm, hbm, hbm],
-            out_specs=[hbm] * 5 + [vmem] * 3,
+            in_specs=[hbm] * 5,
+            out_specs=[hbm] * 8,
             scratch_shapes=[
+                pltpu.VMEM(tokens.shape, jnp.int32), pltpu.VMEM(labels.shape, jnp.int32),
+                pltpu.VMEM((n_stage + 1, 8, tok_n), jnp.int32), pltpu.VMEM((n_stage, tok_n), jnp.int32),
+                pltpu.VMEM((1, tok_n), jnp.int32),
                 pltpu.VMEM((n_stage, dim, ffn), BF16), pltpu.VMEM((n_stage, ffn, dim), BF16),
                 pltpu.VMEM((vocab, dim), BF16), pltpu.VMEM((tok_n, vocab), BF16),
                 pltpu.VMEM((n_stage + 1, tok_n, dim), BF16), pltpu.VMEM((n_stage + 1, tok_n, dim), BF16),
@@ -499,7 +517,7 @@
                 pltpu.VMEM((n_stage, 8, tok_n), F32), pltpu.VMEM((2 * tok_n, dim), F32),
                 pltpu.VMEM((dim, total), BF16), pltpu.VMEM((8, total), F32), pltpu.VMEM((16, total), BF16),
                 pltpu.VMEM((vocab // 2, dim), F32),
-                dma((5,)), dma((14,))] + [dma((n_stage,))] * 12 + [dma((pl.cdiv(vocab // 2, TABLE_BLOCK),))] * 3,
+                dma((8,)), dma((14,))] + [dma((n_stage,))] * 12 + [dma((pl.cdiv(vocab // 2, TABLE_BLOCK),))] * 3,
             compiler_params=pltpu.CompilerParams(collective_id=0, has_side_effects=True, vmem_limit_bytes=VMEM_BYTES),
             name="token_pass",
         )(tokens, labels, emb_table, w_up, w_down)
@@ -510,11 +528,16 @@
             finish_kernel,
             out_shape=[jax.ShapeDtypeStruct((vocab, dim), F32), jax.ShapeDtypeStruct((dim, ffn), F32),
                        jax.ShapeDtypeStruct((ffn, dim), F32), jax.ShapeDtypeStruct((1,), F32)],
-            in_specs=[smem, hbm] + [vmem] * 8, out_specs=[hbm, hbm, hbm, smem],
+            in_specs=[smem] + [hbm] * 9, out_specs=[hbm, hbm, hbm, smem],
             scratch_shapes=[
+                pltpu.VMEM((n_stage, tok_n, dim), BF16), pltpu.VMEM((n_stage, tok_n, dim), BF16),
+                pltpu.VMEM((dim, ffn), BF16), pltpu.VMEM((ffn, dim), BF16), pltpu.VMEM((n_stage, 8, tok_n), F32),
+                pltpu.VMEM((n_stage, tok_n, dim), BF16), pltpu.VMEM((n_stage + 1, 8, tok_n), jnp.int32),
+                pltpu.VMEM((n_stage, tok_n), jnp.int32),
                 pltpu.VMEM((vocab, dim), F32), pltpu.VMEM((n_stage + 1, tok_n, dim), BF16),
                 pltpu.VMEM((total, ffn), BF16), pltpu.VMEM((total, ffn), BF16),
-                pltpu.VMEM((dim, ffn), F32), pltpu.VMEM((ffn, dim), F32), dma((n_blk,)), dma((n_blk,)), dma((2,))],
+                pltpu.VMEM((dim, ffn), F32), pltpu.VMEM((ffn, dim), F32), dma((n_blk,)), dma((n_blk,)), dma((2,)),
+                dma((8,))],
             compiler_params=pltpu.CompilerParams(vmem_limit_bytes=VMEM_BYTES),
             name="finish",
         )(starts, part, xs_all, gs_all, w_up, w_down, st_all, dx_all, ids, rank)

time: 81.6 us -> 73.1 us (0.90)
  Pallas kernels: 80.8 us -> 72.4 us
    pallas_call x1, Pallas kernels: 64.9 us -> 58.2 us  [device_fn(): pl.pallas_call(functools.partial(token_kernel, n_stage), out_shape=[jax.S...]
    pallas_call x1, Pallas kernels: 15.9 us -> 14.2 us  [device_fn(): pl.pallas_call(finish_kernel, out_shape=[jax.ShapeDtypeStruct((vocab, dim...]
where the time goes in v5:
time: 73.1 us
  Pallas kernels  72.4 us (99%)
    pallas_call x1, Pallas kernels, device_fn(): pl.pallas_call(functools.partial(token_kernel, n_stage), out_shape=[jax.S...  58.2 us
    pallas_call x1, Pallas kernels, device_fn(): pl.pallas_call(finish_kernel, out_shape=[jax.ShapeDtypeStruct((vocab, dim...  14.2 us

profile of v5, /device:TPU:81, one launch (start us, length us, event | category | flops | bytes accessed | tf_op | source)
XLA Modules:
  0.0 73.1 jit_solution(3400671447517759617)
XLA Ops:
  0.6 58.2 %token_pass.1 = (f32[8,8,128]{2,1,0:T(8,128)}, bf16[8,128,128]{2,1,0:T(8,128)(2,1)}, bf16[8,128,128]{2,1,0:T(8,128)(2,1)}, bf16[8,128,128]{2,1,0:T(8,128)(2,1)},...) custom-call(s32[16,64]{1,0:T(8,128)} %tok_hbm.1, s32[16,64]{1,0:T(8,128)} %lab_hbm.1, ...), custom_call_target="tpu_custom_call" | custom-call | tf_op jit(solution)/shard_map/token_pass/pallas_call | solution.py:501
  58.8 14.2 %finish.1 = (f32[30592,128]{1,0:T(8,128)}, f32[128,512]{1,0:T(8,128)}, f32[512,128]{1,0:T(8,128)}, f32[1]{0:T(128)}) custom-call(s32[1,128]{1,0:T(1,128)} %get-tuple-element.16.starts_sm, f32[30592,128]{1,0:T(8,128)} %get-tuple-element.17.part_hbm, bf16[8,128,128]{2,1,0:T(8,128)(2,1)} %get-tuple-element.18.x_hbm, ...), custom_call_target="tpu_custom_call" | custom-call | tf_op jit(solution)/shard_map/finish/pallas_call | solution.py:527

commit v6 on v5

--- a/solution.py
+++ b/solution.py
@@ -17,7 +17,8 @@
 HEAD_BLOCK = 4096
 TABLE_BLOCK = 2048
 EMB_BLOCK = 2048
-VMEM_BYTES = 60 * 1024 * 1024
+TOKEN_VMEM = 46 * 1024 * 1024
+FINISH_VMEM = 28 * 1024 * 1024
 
 
 def dot_nn(a, b):
@@ -58,10 +59,10 @@
 
 def token_kernel(
     n_stage, tok_hbm, lab_hbm, emb_hbm, wup_hbm, wdn_hbm,
-    st_out, xs_out, gs_out, dx_out, table_out, ids_hbm, rank_hbm, starts_hbm,
-    tok_ref, lab_ref, ids_out, rank_out, starts_out,
-    wup, wdn, emb, z_buf, xs, gs, pre, n_all, st_all, gat, n_t, level_t, d_lab_t, table,
-    loc_sem, wsend, upr, dnr, xsend, xrecv, gsend, grecv, nsend, nrecv, ssend, srecv, dsend, drecv, tsend, trecv, tloc,
+    st_all, xs_out, gs_out, dx_out, table_out, ids_out, rank_out, wup_out, wdn_out, starts_out,
+    tok_ref, lab_ref,
+    wup, wdn, emb, z_buf, xs, gs, pre, n_all, gat, n_t, level_t, d_lab_t,
+    loc_sem, wsend, upr, dnr, xsend, xrecv, gsend, grecv, nsend, nrecv, ssend, srecv, dsend, drecv, tsend, trecv,
 ):
     me = lax.axis_index("stage")
     n_chip = n_stage // 2
@@ -131,26 +132,24 @@
     starts_out[...] = jnp.sum(acc, axis=0, keepdims=True)
     for i in range(n_stage):
         rank_out[i:i + 1, :] = rank_rows[i]
-    own_i = [pltpu.make_async_copy(ids_out, ids_hbm, loc_sem.at[5]), pltpu.make_async_copy(rank_out, rank_hbm, loc_sem.at[6]),
-             pltpu.make_async_copy(starts_out, starts_hbm, loc_sem.at[7])]
+    wup_out[...] = wup[me]
+    wdn_out[...] = wdn[me]
 
     load_emb.wait()
-    for copy in own_i:
-        copy.start()
     pick = jnp.concatenate(
         [column_of(joined_row(tok_ref, me, tok_n), tok_n), column_of(joined_row(lab_ref, me, tok_n), tok_n)], axis=0)
     lane2 = lax.broadcasted_iota(jnp.int32, (2 * tok_n, tok_n), 1)
 
-    def blocks(body):
-        full = vocab // HEAD_BLOCK
-
+    head_full = vocab // HEAD_BLOCK
+
+    def blocks(body, lo=0, hi=head_full):
         def step(i, carry):
             body(pl.multiple_of(i * HEAD_BLOCK, HEAD_BLOCK), HEAD_BLOCK)
             return carry
 
-        lax.fori_loop(0, full, step, 0)
-        if vocab % HEAD_BLOCK:
-            body(full * HEAD_BLOCK, vocab % HEAD_BLOCK)
+        lax.fori_loop(lo, hi, step, 0)
+        if hi == head_full and vocab % HEAD_BLOCK:
+            body(head_full * HEAD_BLOCK, vocab % HEAD_BLOCK)
 
     gat[...] = jnp.zeros_like(gat)
 
@@ -159,10 +158,7 @@
             [jnp.where(pick == lane2 + (v0 + j * tok_n), 1.0, 0.0).astype(BF16) for j in range(size // tok_n)], axis=1)
         gat[...] += dot_nn(hot, emb[pl.ds(v0, size), :])
 
-    blocks(gather_block)
-    x0 = gat[0:tok_n, :].astype(BF16)
-    lab_rows = gat[tok_n:2 * tok_n, :]
-    lab_bf = lab_rows.astype(BF16)
+    blocks(gather_block, 0, head_full // 2)
 
     up_copy(0, left, sib).wait_recv()
     second = [up_copy(6, left, right), up_copy(7, left, sib)]
@@ -172,6 +168,12 @@
     second += [dn_copy(8, right, left), dn_copy(9, right, sib)]
     second[2].start()
     second[3].start()
+
+    blocks(gather_block, head_full // 2, head_full)
+    x0 = gat[0:tok_n, :].astype(BF16)
+    lab_rows = gat[tok_n:2 * tok_n, :]
+    lab_bf = lab_rows.astype(BF16)
+
     dn_copy(0, left, sib).wait_recv()
     second.append(dn_copy(10, left, sib))
     second[4].start()
@@ -193,8 +195,6 @@
         return pltpu.make_async_remote_copy(
             gs.at[layer + 1], gs_out.at[me], gsend.at[layer], grecv.at[me], device_id={"stage": layer}, device_id_type=MESH)
 
-    own_x = pltpu.make_async_copy(xs.at[me], xs_out.at[me], loc_sem.at[0])
-    own_g = pltpu.make_async_copy(gs.at[me + 1], gs_out.at[me], loc_sem.at[1])
 
     xs[0] = x0
 
@@ -216,7 +216,7 @@
 
         @pl.when(layer == me)
         def _():
-            own_x.start()
+            xs_out[me] = x
 
         return carry
 
@@ -294,7 +294,7 @@
 
         @pl.when(layer == me)
         def _():
-            own_g.start()
+            gs_out[me] = g
 
         return carry
 
@@ -302,15 +302,12 @@
     send_d = spread(gs.at[0], dx_out, dsend, drecv)
     for copy in send_d:
         copy.start()
-    own_d = pltpu.make_async_copy(gs.at[0], dx_out.at[me], loc_sem.at[4])
-    own_d.start()
+    dx_out[me] = gs[0]
 
     for peer in peers:
         for buf, send, recv in ((n_all, nsend, nrecv), (st_all, ssend, srecv)):
             pltpu.make_async_remote_copy(buf.at[peer], buf.at[peer], send.at[0], recv.at[peer],
                                          device_id={"stage": peer}, device_id_type=MESH).wait_recv()
-    own_s = pltpu.make_async_copy(st_all, st_out, loc_sem.at[3])
-    own_s.start()
     for i in range(n_stage):
         cols = slice(i * tok_n, (i + 1) * tok_n)
         n_t[:, cols] = jnp.transpose(n_all[i])
@@ -320,11 +317,9 @@
     wide = 2 * tok_n
 
     def table_copies(j, size):
-        local = pl.ds(pl.multiple_of(j * TABLE_BLOCK, 16), size)
         rows = pl.ds(pl.multiple_of(core * half + j * TABLE_BLOCK, 16), size)
-        return (pltpu.make_async_remote_copy(table.at[local], table_out.at[rows], tsend.at[j], trecv.at[j],
-                                             device_id={"stage": sib}, device_id_type=MESH),
-                pltpu.make_async_copy(table.at[local], table_out.at[rows], tloc.at[j]))
+        return (pltpu.make_async_remote_copy(table_out.at[rows], table_out.at[rows], tsend.at[j], trecv.at[j],
+                                             device_id={"stage": sib}, device_id_type=MESH),)
 
     def table_start(j, size):
         for copy in table_copies(j, size):
@@ -343,7 +338,7 @@
             lab = jnp.broadcast_to(lab, (16, wide)).astype(jnp.int16)
             dz = jnp.where(row16 == lab[0:1, :], d_lab_t[0:1, cols], p)
             acc = acc + dot_nn(dz, jnp.concatenate([n_all[2 * t], n_all[2 * t + 1]], axis=0))
-        table[pl.ds(pl.multiple_of(j * TABLE_BLOCK, 16), size), :] = acc * scale
+        table_out[pl.ds(base, size), :] = acc * scale
 
     full, tail = half // TABLE_BLOCK, half % TABLE_BLOCK
 
@@ -362,8 +357,6 @@
 
     for copy in first + second + send_n + send_s:
         copy.wait_send()
-    for copy in (own_x, own_g, own_s, own_d, *own_i):
-        copy.wait()
     for peer in peers:
         pltpu.make_async_remote_copy(xs.at[peer], xs_out.at[peer], xsend.at[peer], xrecv.at[peer],
                                      device_id={"stage": peer}, device_id_type=MESH).wait()
@@ -377,11 +370,9 @@
         table_start(full, tail)
 
     def table_wait(j, size):
-        remote, local = table_copies(j, size)
-        remote.wait_send()
-        local.wait()
+        table_copies(j, size)[0].wait_send()
         rows = pl.ds(pl.multiple_of((1 - core) * half + j * TABLE_BLOCK, 16), size)
-        pltpu.make_async_remote_copy(table.at[pl.ds(pl.multiple_of(j * TABLE_BLOCK, 16), size)], table_out.at[rows],
+        pltpu.make_async_remote_copy(table_out.at[rows], table_out.at[rows],
                                      tsend.at[j], trecv.at[j], device_id={"stage": sib}, device_id_type=MESH).wait_recv()
 
     def wait_step(j, carry):
@@ -394,10 +385,9 @@
 
 
 def finish_kernel(
-    starts_sm, part_hbm, x_hbm, g_hbm, wup_hbm, wdn_hbm, st_hbm, dx_hbm, ids_hbm, rank_hbm,
+    starts_ref, part_ref, x_ref, g_ref, wup_ref, wdn_ref, st_ref, dx_ref, ids_ref, rank_ref,
     out_hbm, gup_hbm, gdn_hbm, loss_ref,
-    x_ref, g_ref, wup_ref, wdn_ref, st_ref, dx_ref, ids_ref, rank_ref,
-    buf, dxs, hid, da, gup, gdn, read_sem, write_sem, grad_sem, load_sem,
+    starts_sm, buf, dxs, hid, da, gup, gdn, write_sem, grad_sem,
 ):
     n_chunk, tok_n, dim = dx_ref.shape
     vocab = buf.shape[0]
@@ -407,9 +397,6 @@
     def span(j, size):
         return pl.ds(pl.multiple_of(j * EMB_BLOCK, 16), size)
 
-    def read(j, size):
-        return pltpu.make_async_copy(part_hbm.at[span(j, size)], buf.at[span(j, size)], read_sem.at[j])
-
     def write(j, size):
         return pltpu.make_async_copy(buf.at[span(j, size)], out_hbm.at[span(j, size)], write_sem.at[j])
 
@@ -422,14 +409,8 @@
         if tail:
             fn(full, tail)
 
-    loads = [pltpu.make_async_copy(src, dst, load_sem.at[i]) for i, (src, dst) in enumerate((
-        (x_hbm, x_ref), (wup_hbm, wup_ref), (g_hbm, g_ref), (wdn_hbm, wdn_ref), (st_hbm, st_ref), (dx_hbm, dx_ref),
-        (ids_hbm, ids_ref), (rank_hbm, rank_ref)))]
-    for copy in loads:
-        copy.start()
-    each(lambda j, size: read(j, size).start())
-    for copy in loads:
-        copy.wait()
+    load_starts = pltpu.make_async_copy(starts_ref, starts_sm, grad_sem.at[2])
+    load_starts.start()
 
     step_n = 2 * tok_n
     for i in range(n_chunk // 2):
@@ -460,7 +441,6 @@
     dxs[n_chunk] = jnp.zeros((tok_n, dim), BF16)
 
     def add_tokens(j, size):
-        read(j, size).wait()
         rows = span(j, size)
         row16 = lax.broadcasted_iota(jnp.int16, (size, tok_n), 0)
 
@@ -470,7 +450,7 @@
 
         first = jnp.minimum(starts_sm[0, j] // tok_n, n_chunk - 1)
         last = (starts_sm[0, j + 1] + tok_n - 1) // tok_n
-        buf[rows, :] += dot_nn(jnp.concatenate([hot_rows(first), hot_rows(first + 1)], axis=1),
+        buf[rows, :] = part_ref[rows, :] + dot_nn(jnp.concatenate([hot_rows(first), hot_rows(first + 1)], axis=1),
                                jnp.concatenate([dxs[first], dxs[first + 1]], axis=0))
 
         def more(c, carry):
@@ -480,6 +460,7 @@
         lax.fori_loop(first + 2, last, more, 0)
         write(j, size).start()
 
+    load_starts.wait()
     each(add_tokens)
     each(lambda j, size: write(j, size).wait())
     for copy in grads:
@@ -496,29 +477,27 @@
         tok_n = total // n_stage
         w_up, w_down = w_up[0], w_down[0]
         hbm = pl.BlockSpec(memory_space=pl.ANY)
+        vmem = pl.BlockSpec(memory_space=pltpu.VMEM)
         dma = pltpu.SemaphoreType.DMA
-        act = jax.ShapeDtypeStruct((n_stage, tok_n, dim), BF16)
-        st_all, xs_all, gs_all, dx_all, part, ids, rank, starts = pl.pallas_call(
+        act = pltpu.VMEM((n_stage, tok_n, dim), BF16)
+        st_all, xs_all, gs_all, dx_all, part, ids, rank, wup_own, wdn_own, starts = pl.pallas_call(
             functools.partial(token_kernel, n_stage),
-            out_shape=[jax.ShapeDtypeStruct((n_stage, 8, tok_n), F32), act, act, act,
-                       jax.ShapeDtypeStruct((vocab, dim), F32),
-                       jax.ShapeDtypeStruct((n_stage + 1, 8, tok_n), jnp.int32),
-                       jax.ShapeDtypeStruct((n_stage, tok_n), jnp.int32), jax.ShapeDtypeStruct((1, tok_n), jnp.int32)],
+            out_shape=[pltpu.VMEM((n_stage, 8, tok_n), F32), act, act, act, pltpu.VMEM((vocab, dim), F32),
+                       pltpu.VMEM((n_stage + 1, 8, tok_n), jnp.int32), pltpu.VMEM((n_stage, tok_n), jnp.int32),
+                       pltpu.VMEM((dim, ffn), BF16), pltpu.VMEM((ffn, dim), BF16),
+                       pltpu.VMEM((1, tok_n), jnp.int32)],
             in_specs=[hbm] * 5,
-            out_specs=[hbm] * 8,
+            out_specs=[vmem] * 10,
             scratch_shapes=[
                 pltpu.VMEM(tokens.shape, jnp.int32), pltpu.VMEM(labels.shape, jnp.int32),
-                pltpu.VMEM((n_stage + 1, 8, tok_n), jnp.int32), pltpu.VMEM((n_stage, tok_n), jnp.int32),
-                pltpu.VMEM((1, tok_n), jnp.int32),
                 pltpu.VMEM((n_stage, dim, ffn), BF16), pltpu.VMEM((n_stage, ffn, dim), BF16),
                 pltpu.VMEM((vocab, dim), BF16), pltpu.VMEM((tok_n, vocab), BF16),
                 pltpu.VMEM((n_stage + 1, tok_n, dim), BF16), pltpu.VMEM((n_stage + 1, tok_n, dim), BF16),
                 pltpu.VMEM((n_stage, tok_n, ffn), BF16), pltpu.VMEM((n_stage, tok_n, dim), BF16),
-                pltpu.VMEM((n_stage, 8, tok_n), F32), pltpu.VMEM((2 * tok_n, dim), F32),
+                pltpu.VMEM((2 * tok_n, dim), F32),
                 pltpu.VMEM((dim, total), BF16), pltpu.VMEM((8, total), F32), pltpu.VMEM((16, total), BF16),
-                pltpu.VMEM((vocab // 2, dim), F32),
-                dma((8,)), dma((14,))] + [dma((n_stage,))] * 12 + [dma((pl.cdiv(vocab // 2, TABLE_BLOCK),))] * 3,
-            compiler_params=pltpu.CompilerParams(collective_id=0, has_side_effects=True, vmem_limit_bytes=VMEM_BYTES),
+                dma((5,)), dma((14,))] + [dma((n_stage,))] * 12 + [dma((pl.cdiv(vocab // 2, TABLE_BLOCK),))] * 2,
+            compiler_params=pltpu.CompilerParams(collective_id=0, has_side_effects=True, vmem_limit_bytes=TOKEN_VMEM),
             name="token_pass",
         )(tokens, labels, emb_table, w_up, w_down)
 
@@ -528,19 +507,15 @@
             finish_kernel,
             out_shape=[jax.ShapeDtypeStruct((vocab, dim), F32), jax.ShapeDtypeStruct((dim, ffn), F32),
                        jax.ShapeDtypeStruct((ffn, dim), F32), jax.ShapeDtypeStruct((1,), F32)],
-            in_specs=[smem] + [hbm] * 9, out_specs=[hbm, hbm, hbm, smem],
+            in_specs=[vmem] * 10, out_specs=[hbm, hbm, hbm, smem],
             scratch_shapes=[
-                pltpu.VMEM((n_stage, tok_n, dim), BF16), pltpu.VMEM((n_stage, tok_n, dim), BF16),
-                pltpu.VMEM((dim, ffn), BF16), pltpu.VMEM((ffn, dim), BF16), pltpu.VMEM((n_stage, 8, tok_n), F32),
-                pltpu.VMEM((n_stage, tok_n, dim), BF16), pltpu.VMEM((n_stage + 1, 8, tok_n), jnp.int32),
-                pltpu.VMEM((n_stage, tok_n), jnp.int32),
+                pltpu.SMEM((1, tok_n), jnp.int32),
                 pltpu.VMEM((vocab, dim), F32), pltpu.VMEM((n_stage + 1, tok_n, dim), BF16),
                 pltpu.VMEM((total, ffn), BF16), pltpu.VMEM((total, ffn), BF16),
-                pltpu.VMEM((dim, ffn), F32), pltpu.VMEM((ffn, dim), F32), dma((n_blk,)), dma((n_blk,)), dma((2,)),
-                dma((8,))],
-            compiler_params=pltpu.CompilerParams(vmem_limit_bytes=VMEM_BYTES),
+                pltpu.VMEM((dim, ffn), F32), pltpu.VMEM((ffn, dim), F32), dma((n_blk,)), dma((3,))],
+            compiler_params=pltpu.CompilerParams(vmem_limit_bytes=FINISH_VMEM),
             name="finish",
-        )(starts, part, xs_all, gs_all, w_up, w_down, st_all, dx_all, ids, rank)
+        )(starts, part, xs_all, gs_all, wup_own, wdn_own, st_all, dx_all, ids, rank)
         return loss, grad_up[None], grad_down[None], grad_emb
 
     return jax.shard_map(

time: 73.1 us -> 68.4 us (0.936)
  Pallas kernels: 72.4 us -> 67.7 us
    pallas_call x1, Pallas kernels: 58.2 us -> 55.7 us  [device_fn(): pl.pallas_call(functools.partial(token_kernel, n_stage), out_shape=[pltpu...]
    pallas_call x1, Pallas kernels: 14.2 us -> 12 us  [device_fn(): pl.pallas_call(finish_kernel, out_shape=[jax.ShapeDtypeStruct((vocab, dim...]
where the time goes in v6:
time: 68.4 us
  Pallas kernels  67.7 us (99%)
    pallas_call x1, Pallas kernels, device_fn(): pl.pallas_call(functools.partial(token_kernel, n_stage), out_shape=[pltpu...  55.7 us
    pallas_call x1, Pallas kernels, device_fn(): pl.pallas_call(finish_kernel, out_shape=[jax.ShapeDtypeStruct((vocab, dim...  12 us

profile of v6, /device:TPU:81, one launch (start us, length us, event | category | flops | bytes accessed | tf_op | source)
XLA Modules:
  0.0 68.4 jit_solution(11803585363762108010)
XLA Ops:
  0.6 55.7 %token_pass.1 = (f32[8,8,128]{2,1,0:T(8,128)S(1)}, bf16[8,128,128]{2,1,0:T(8,128)(2,1)S(1)}, bf16[8,128,128]{2,1,0:T(8,128)(2,1)S(1)}, bf16[8,128,128]{2,1,0:T(8...) custom-call(s32[16,64]{1,0:T(8,128)} %tok_hbm.1, ...), custom_call_target="tpu_custom_call" | custom-call | tf_op jit(solution)/shard_map/token_pass/pallas_call | solution.py:483
  56.3 12.0 %finish.1 = (f32[30592,128]{1,0:T(8,128)}, f32[128,512]{1,0:T(8,128)}, f32[512,128]{1,0:T(8,128)}, f32[1]{0:T(128)}) custom-call(s32[1,128]{1,0:T(1,128)S(1)} %get-tuple-element.18.starts_ref, f32[30592,128]{1,0:T(8,128)S(1)} %get-tuple-element.19.part_ref, bf16[8,128,128]{2,1,0:T(8,128)(2,1)S(1)} %get-tuple-element.20.x_ref, ...), custom_call_target="tpu_custom_call" | custom-call | tf_op jit(solution)/shard_map/finish/pallas_call | solution.py:506

commit v7 on v6

--- a/solution.py
+++ b/solution.py
@@ -59,8 +59,8 @@
 
 def token_kernel(
     n_stage, tok_hbm, lab_hbm, emb_hbm, wup_hbm, wdn_hbm,
-    st_all, xs_out, gs_out, dx_out, table_out, ids_out, rank_out, wup_out, wdn_out, starts_out,
-    tok_ref, lab_ref,
+    st_all, table_out, ids_out, starts_out, dxs, gup_out, gdn_out,
+    tok_ref, lab_ref, rank_out, xs_out, gs_out, dx_out, hid, da_buf,
     wup, wdn, emb, z_buf, xs, gs, pre, n_all, gat, n_t, level_t, d_lab_t,
     loc_sem, wsend, upr, dnr, xsend, xrecv, gsend, grecv, nsend, nrecv, ssend, srecv, dsend, drecv, tsend, trecv,
 ):
@@ -132,8 +132,6 @@
     starts_out[...] = jnp.sum(acc, axis=0, keepdims=True)
     for i in range(n_stage):
         rank_out[i:i + 1, :] = rank_rows[i]
-    wup_out[...] = wup[me]
-    wdn_out[...] = wdn[me]
 
     load_emb.wait()
     pick = jnp.concatenate(
@@ -281,24 +279,28 @@
     corr = jnp.mean(dn * x_last, axis=-1, keepdims=True)
     gs[n_stage] = (inv * dn - x_last * (inv * inv * inv * corr)).astype(BF16)
 
-    def backward(i, carry):
-        layer = n_stage - 1 - i
+    def backward(layer):
         g = gs[layer + 1]
         dh = dot_nt(g, wdn[layer]).astype(BF16).astype(F32)
         da = (dh * gelu_slope(pre[layer].astype(F32))).astype(BF16)
         gs[layer] = (g.astype(F32) + dot_nt(da, wup[layer])).astype(BF16)
 
+    def send_g(layer):
         @pl.when(layer != me)
         def _():
             g_copy(layer).start()
 
         @pl.when(layer == me)
         def _():
-            gs_out[me] = g
-
+            gs_out[me] = gs[layer + 1]
+
+    def back_step(i, carry):
+        layer = n_stage - 1 - i
+        backward(layer)
+        send_g(layer)
         return carry
 
-    lax.fori_loop(0, n_stage, backward, 0)
+    lax.fori_loop(0, n_stage, back_step, 0)
     send_d = spread(gs.at[0], dx_out, dsend, drecv)
     for copy in send_d:
         copy.start()
@@ -341,6 +343,7 @@
         table_out[pl.ds(base, size), :] = acc * scale
 
     full, tail = half // TABLE_BLOCK, half % TABLE_BLOCK
+    grad_tok = 2 * tok_n
 
     def table_step(j, carry):
         @pl.when(j > 0)
@@ -354,9 +357,8 @@
     table_start(full - 1, TABLE_BLOCK)
     if tail:
         table_block(full, tail)
-
-    for copy in first + second + send_n + send_s:
-        copy.wait_send()
+        table_start(full, tail)
+
     for peer in peers:
         pltpu.make_async_remote_copy(xs.at[peer], xs_out.at[peer], xsend.at[peer], xrecv.at[peer],
                                      device_id={"stage": peer}, device_id_type=MESH).wait()
@@ -364,10 +366,37 @@
                                      device_id={"stage": peer}, device_id_type=MESH).wait()
         pltpu.make_async_remote_copy(gs.at[0], dx_out.at[peer], dsend.at[0], drecv.at[peer],
                                      device_id={"stage": peer}, device_id_type=MESH).wait_recv()
+
+    def weight_part(i):
+        x = jnp.concatenate([xs_out[2 * i], xs_out[2 * i + 1]], axis=0)
+        g = jnp.concatenate([gs_out[2 * i], gs_out[2 * i + 1]], axis=0)
+        a = dot_nn(x, wup[me]).astype(BF16).astype(F32)
+        sq = a * a
+        t = jnp.tanh(GELU_C * (a + 0.044715 * (sq * a)))
+        cdf = 0.5 * (1.0 + t)
+        rows = slice(i * grad_tok, (i + 1) * grad_tok)
+        hid[rows, :] = (a * cdf).astype(BF16)
+        slope = cdf + (0.5 * a) * (1.0 - t * t) * (GELU_C * (1.0 + (3.0 * 0.044715) * sq))
+        dh = dot_nt(g, wdn[me]).astype(BF16).astype(F32)
+        da_buf[rows, :] = (dh * slope).astype(BF16)
+
+    for i in range(n_stage // 2):
+        weight_part(i)
+    gup_out[...] = dot_tn(xs_out[...].reshape(total, dim), da_buf[...])
+    gdn_out[...] = jnp.transpose(dot_tn(gs_out[...].reshape(total, dim), hid[...]))
+    row_id = lax.broadcasted_iota(jnp.int32, (tok_n, tok_n), 0)
+    for c in range(n_stage):
+        acc = jnp.zeros((tok_n, dim), F32)
+        for i in range(n_stage):
+            hot = jnp.where(rank_out[i:i + 1, :] == row_id + c * tok_n, 1.0, 0.0).astype(BF16)
+            acc = acc + dot_nn(hot, dx_out[i])
+        dxs[c] = acc.astype(BF16)
+    dxs[n_stage] = jnp.zeros((tok_n, dim), BF16)
+
+    for copy in first + second + send_n + send_s:
+        copy.wait_send()
     for copy in send_d:
         copy.wait_send()
-    if tail:
-        table_start(full, tail)
 
     def table_wait(j, size):
         table_copies(j, size)[0].wait_send()
@@ -385,13 +414,13 @@
 
 
 def finish_kernel(
-    starts_ref, part_ref, x_ref, g_ref, wup_ref, wdn_ref, st_ref, dx_ref, ids_ref, rank_ref,
+    starts_ref, part_ref, st_ref, ids_ref, dxs, gup_ref, gdn_ref,
     out_hbm, gup_hbm, gdn_hbm, loss_ref,
-    starts_sm, buf, dxs, hid, da, gup, gdn, write_sem, grad_sem,
+    starts_sm, buf, write_sem, grad_sem,
 ):
-    n_chunk, tok_n, dim = dx_ref.shape
+    n_chunk, tok_n, _ = dxs.shape
+    n_chunk = n_chunk - 1
     vocab = buf.shape[0]
-    ffn = hid.shape[1]
     full, tail = vocab // EMB_BLOCK, vocab % EMB_BLOCK
 
     def span(j, size):
@@ -412,33 +441,10 @@
     load_starts = pltpu.make_async_copy(starts_ref, starts_sm, grad_sem.at[2])
     load_starts.start()
 
-    step_n = 2 * tok_n
-    for i in range(n_chunk // 2):
-        x = jnp.concatenate([x_ref[2 * i], x_ref[2 * i + 1]], axis=0)
-        g = jnp.concatenate([g_ref[2 * i], g_ref[2 * i + 1]], axis=0)
-        a = dot_nn(x, wup_ref[...]).astype(BF16).astype(F32)
-        sq = a * a
-        t = jnp.tanh(GELU_C * (a + 0.044715 * (sq * a)))
-        cdf = 0.5 * (1.0 + t)
-        hid[i * step_n:(i + 1) * step_n, :] = (a * cdf).astype(BF16)
-        slope = cdf + (0.5 * a) * (1.0 - t * t) * (GELU_C * (1.0 + (3.0 * 0.044715) * sq))
-        dh = dot_nt(g, wdn_ref[...]).astype(BF16).astype(F32)
-        da[i * step_n:(i + 1) * step_n, :] = (dh * slope).astype(BF16)
-    gup[...] = dot_tn(x_ref[...].reshape(n_chunk * tok_n, dim), da[...])
-    gdn[...] = jnp.transpose(dot_tn(g_ref[...].reshape(n_chunk * tok_n, dim), hid[...]))
-    grads = [pltpu.make_async_copy(gup, gup_hbm, grad_sem.at[0]), pltpu.make_async_copy(gdn, gdn_hbm, grad_sem.at[1])]
+    grads = [pltpu.make_async_copy(gup_ref, gup_hbm, grad_sem.at[0]), pltpu.make_async_copy(gdn_ref, gdn_hbm, grad_sem.at[1])]
     for copy in grads:
         copy.start()
     loss_ref[0] = jnp.sum(st_ref[:, 2, :]) * (1.0 / (n_chunk * tok_n))
-
-    row_id = lax.broadcasted_iota(jnp.int32, (tok_n, tok_n), 0)
-    for c in range(n_chunk):
-        acc = jnp.zeros((tok_n, dim), F32)
-        for i in range(n_chunk):
-            hot = jnp.where(rank_ref[i:i + 1, :] == row_id + c * tok_n, 1.0, 0.0).astype(BF16)
-            acc = acc + dot_nn(hot, dx_ref[i])
-        dxs[c] = acc.astype(BF16)
-    dxs[n_chunk] = jnp.zeros((tok_n, dim), BF16)
 
     def add_tokens(j, size):
         rows = span(j, size)
@@ -480,16 +486,16 @@
         vmem = pl.BlockSpec(memory_space=pltpu.VMEM)
         dma = pltpu.SemaphoreType.DMA
         act = pltpu.VMEM((n_stage, tok_n, dim), BF16)
-        st_all, xs_all, gs_all, dx_all, part, ids, rank, wup_own, wdn_own, starts = pl.pallas_call(
+        st_all, part, ids, starts, dxs, gup, gdn = pl.pallas_call(
             functools.partial(token_kernel, n_stage),
-            out_shape=[pltpu.VMEM((n_stage, 8, tok_n), F32), act, act, act, pltpu.VMEM((vocab, dim), F32),
-                       pltpu.VMEM((n_stage + 1, 8, tok_n), jnp.int32), pltpu.VMEM((n_stage, tok_n), jnp.int32),
-                       pltpu.VMEM((dim, ffn), BF16), pltpu.VMEM((ffn, dim), BF16),
-                       pltpu.VMEM((1, tok_n), jnp.int32)],
+            out_shape=[pltpu.VMEM((n_stage, 8, tok_n), F32), pltpu.VMEM((vocab, dim), F32),
+                       pltpu.VMEM((n_stage + 1, 8, tok_n), jnp.int32), pltpu.VMEM((1, tok_n), jnp.int32),
+                       pltpu.VMEM((n_stage + 1, tok_n, dim), BF16), pltpu.VMEM((dim, ffn), F32), pltpu.VMEM((ffn, dim), F32)],
             in_specs=[hbm] * 5,
-            out_specs=[vmem] * 10,
+            out_specs=[vmem] * 7,
             scratch_shapes=[
-                pltpu.VMEM(tokens.shape, jnp.int32), pltpu.VMEM(labels.shape, jnp.int32),
+                pltpu.VMEM(tokens.shape, jnp.int32), pltpu.VMEM(labels.shape, jnp.int32), pltpu.VMEM((n_stage, tok_n), jnp.int32),
+                act, act, act, pltpu.VMEM((total, ffn), BF16), pltpu.VMEM((total, ffn), BF16),
                 pltpu.VMEM((n_stage, dim, ffn), BF16), pltpu.VMEM((n_stage, ffn, dim), BF16),
                 pltpu.VMEM((vocab, dim), BF16), pltpu.VMEM((tok_n, vocab), BF16),
                 pltpu.VMEM((n_stage + 1, tok_n, dim), BF16), pltpu.VMEM((n_stage + 1, tok_n, dim), BF16),
@@ -507,15 +513,12 @@
             finish_kernel,
             out_shape=[jax.ShapeDtypeStruct((vocab, dim), F32), jax.ShapeDtypeStruct((dim, ffn), F32),
                        jax.ShapeDtypeStruct((ffn, dim), F32), jax.ShapeDtypeStruct((1,), F32)],
-            in_specs=[vmem] * 10, out_specs=[hbm, hbm, hbm, smem],
+            in_specs=[vmem] * 7, out_specs=[hbm, hbm, hbm, smem],
             scratch_shapes=[
-                pltpu.SMEM((1, tok_n), jnp.int32),
-                pltpu.VMEM((vocab, dim), F32), pltpu.VMEM((n_stage + 1, tok_n, dim), BF16),
-                pltpu.VMEM((total, ffn), BF16), pltpu.VMEM((total, ffn), BF16),
-                pltpu.VMEM((dim, ffn), F32), pltpu.VMEM((ffn, dim), F32), dma((n_blk,)), dma((3,))],
+                pltpu.SMEM((1, tok_n), jnp.int32), pltpu.VMEM((vocab, dim), F32), dma((n_blk,)), dma((3,))],
             compiler_params=pltpu.CompilerParams(vmem_limit_bytes=FINISH_VMEM),
             name="finish",
-        )(starts, part, xs_all, gs_all, wup_own, wdn_own, st_all, dx_all, ids, rank)
+        )(starts, part, st_all, ids, dxs, gup, gdn)
         return loss, grad_up[None], grad_down[None], grad_emb
 
     return jax.shard_map(

time: 68.4 us -> 67.2 us (0.982)
  Pallas kernels: 67.7 us -> 66.5 us
    pallas_call x1, Pallas kernels: 12 us -> 9.94 us  [device_fn(): pl.pallas_call(finish_kernel, out_shape=[jax.ShapeDtypeStruct((vocab, dim...]
    pallas_call x1, Pallas kernels: 55.7 us -> 56.6 us  [device_fn(): pl.pallas_call(functools.partial(token_kernel, n_stage), out_shape=[pltpu...]
where the time goes in v7:
time: 67.2 us; the launch traced here: 67.1 us
  Pallas kernels  66.5 us (99%)
    pallas_call x1, Pallas kernels, device_fn(): pl.pallas_call(functools.partial(token_kernel, n_stage), out_shape=[pltpu...  56.6 us
    pallas_call x1, Pallas kernels, device_fn(): pl.pallas_call(finish_kernel, out_shape=[jax.ShapeDtypeStruct((vocab, dim...  9.94 us

profile of v7, /device:TPU:81, one launch (start us, length us, event | category | flops | bytes accessed | tf_op | source)
XLA Modules:
  0.0 67.1 jit_solution(14314409514480145723)
XLA Ops:
  0.6 56.6 %token_pass.1 = (f32[8,8,128]{2,1,0:T(8,128)S(1)}, f32[30592,128]{1,0:T(8,128)S(1)}, s32[9,8,128]{2,1,0:T(8,128)S(1)}, s32[1,128]{1,0:T(1,128)S(1)}, bf16[9,128,...) custom-call(s32[16,64]{1,0:T(8,128)} %tok_hbm.1, s32[16,64]{1,0:T(8,128)} %lab_hbm.1, ...), custom_call_target="tpu_custom_call" | custom-call | tf_op jit(solution)/shard_map/token_pass/pallas_call | solution.py:489
  57.2 9.9 %finish.1 = (f32[30592,128]{1,0:T(8,128)}, f32[128,512]{1,0:T(8,128)}, f32[512,128]{1,0:T(8,128)}, f32[1]{0:T(128)}) custom-call(s32[1,128]{1,0:T(1,128)S(1)} %get-tuple-element.15.starts_ref, f32[30592,128]{1,0:T(8,128)S(1)} %get-tuple-element.16.part_ref, f32[8,8,128]{2,1,0:T(8,128)S(1)} %get-tuple-element.17.st_ref, ...), custom_call_target="tpu_custom_call" | custom-call | tf_op jit(solution)/shard_map/finish/pallas_call | solution.py:512

commit v8 on v7

--- a/solution.py
+++ b/solution.py
@@ -14,9 +14,10 @@
 LOG2E = math.log2(math.e)
 LN2 = math.log(2.0)
 GELU_C = math.sqrt(2.0 / math.pi)
-HEAD_BLOCK = 4096
-TABLE_BLOCK = 2048
+HEAD_BLOCK = 8192
+TABLE_BLOCK = 3648
 EMB_BLOCK = 2048
+WRITE_PARTS = 4
 TOKEN_VMEM = 46 * 1024 * 1024
 FINISH_VMEM = 28 * 1024 * 1024
 
@@ -329,18 +330,22 @@
 
     def table_block(j, size):
         base = pl.multiple_of(core * half + j * TABLE_BLOCK, 16)
-        e = emb[pl.ds(base, size), :]
+        for r in range(0, size, 608):
+            table_rows(base, j * TABLE_BLOCK + r, r, min(608, size - r))
+
+    def table_rows(base, at, r, size):
+        e = emb[pl.ds(pl.multiple_of(base + r, 16), size), :]
         row16 = lax.broadcasted_iota(jnp.int16, (size, wide), 0)
         acc = jnp.zeros((size, dim), F32)
         for t in range(total // wide):
             cols = slice(t * wide, (t + 1) * wide)
             z = (dot_nn(e, n_t[:, cols]) * scale).astype(BF16).astype(F32)
             p = jnp.exp2(z * LOG2E - level_t[0:1, cols]).astype(BF16)
-            lab = jnp.concatenate([joined_row(lab_ref, 2 * t, tok_n), joined_row(lab_ref, 2 * t + 1, tok_n)], axis=1) - base
+            lab = jnp.concatenate([joined_row(lab_ref, 2 * t, tok_n), joined_row(lab_ref, 2 * t + 1, tok_n)], axis=1) - (base + r)
             lab = jnp.broadcast_to(lab, (16, wide)).astype(jnp.int16)
             dz = jnp.where(row16 == lab[0:1, :], d_lab_t[0:1, cols], p)
             acc = acc + dot_nn(dz, jnp.concatenate([n_all[2 * t], n_all[2 * t + 1]], axis=0))
-        table_out[pl.ds(base, size), :] = acc * scale
+        table_out[pl.ds(pl.multiple_of(base + r, 16), size), :] = acc * scale
 
     full, tail = half // TABLE_BLOCK, half % TABLE_BLOCK
     grad_tok = 2 * tok_n
@@ -427,7 +432,18 @@
         return pl.ds(pl.multiple_of(j * EMB_BLOCK, 16), size)
 
     def write(j, size):
-        return pltpu.make_async_copy(buf.at[span(j, size)], out_hbm.at[span(j, size)], write_sem.at[j])
+        part = size // WRITE_PARTS
+        return [pltpu.make_async_copy(
+            buf.at[pl.ds(pl.multiple_of(j * EMB_BLOCK + k * part, 8), part)],
+            out_hbm.at[pl.ds(pl.multiple_of(j * EMB_BLOCK + k * part, 8), part)], write_sem.at[j, k]) for k in range(WRITE_PARTS)]
+
+    def write_start(j, size):
+        for k, copy in enumerate(write(j, size)):
+            copy.start(priority=k % 2)
+
+    def write_wait(j, size):
+        for copy in write(j, size):
+            copy.wait()
 
     def each(fn):
         def step(j, carry):
@@ -464,11 +480,11 @@
             return carry
 
         lax.fori_loop(first + 2, last, more, 0)
-        write(j, size).start()
+        write_start(j, size)
 
     load_starts.wait()
     each(add_tokens)
-    each(lambda j, size: write(j, size).wait())
+    each(write_wait)
     for copy in grads:
         copy.wait()
 
@@ -515,7 +531,7 @@
                        jax.ShapeDtypeStruct((ffn, dim), F32), jax.ShapeDtypeStruct((1,), F32)],
             in_specs=[vmem] * 7, out_specs=[hbm, hbm, hbm, smem],
             scratch_shapes=[
-                pltpu.SMEM((1, tok_n), jnp.int32), pltpu.VMEM((vocab, dim), F32), dma((n_blk,)), dma((3,))],
+                pltpu.SMEM((1, tok_n), jnp.int32), pltpu.VMEM((vocab, dim), F32), dma((n_blk, WRITE_PARTS)), dma((3,))],
             compiler_params=pltpu.CompilerParams(vmem_limit_bytes=FINISH_VMEM),
             name="finish",
         )(starts, part, st_all, ids, dxs, gup, gdn)

time: 67.2 us -> 64.8 us (0.964)
  Pallas kernels: 66.5 us -> 63.8 us
    pallas_call x1, Pallas kernels: 56.6 us -> 53.5 us  [device_fn(): pl.pallas_call(functools.partial(token_kernel, n_stage), out_shape=[pltpu...]
where the time goes in v8:
time: 64.8 us; the launch traced here: 64.7 us
  Pallas kernels  63.8 us (98%)
  between operations  0.82 us (1%)
    pallas_call x1, Pallas kernels, device_fn(): pl.pallas_call(functools.partial(token_kernel, n_stage), out_shape=[pltpu...  53.5 us
    pallas_call x1, Pallas kernels, device_fn(): pl.pallas_call(finish_kernel, out_shape=[jax.ShapeDtypeStruct((vocab, dim...  10.3 us

profile of v8, /device:TPU:81, one launch (start us, length us, event | category | flops | bytes accessed | tf_op | source)
XLA Modules:
  0.0 64.7 jit_solution(10928778770756951075)
XLA Ops:
  0.6 53.5 %token_pass.1 = (f32[8,8,128]{2,1,0:T(8,128)S(1)}, f32[30592,128]{1,0:T(8,128)S(1)}, s32[9,8,128]{2,1,0:T(8,128)S(1)}, s32[1,128]{1,0:T(1,128)S(1)}, bf16[9,128,...) custom-call(s32[16,64]{1,0:T(8,128)} %tok_hbm.1, s32[16,64]{1,0:T(8,128)} %lab_hbm.1, ...), custom_call_target="tpu_custom_call" | custom-call | tf_op jit(solution)/shard_map/token_pass/pallas_call | solution.py:505
  54.2 10.3 %finish.1 = (f32[30592,128]{1,0:T(8,128)}, f32[128,512]{1,0:T(8,128)}, f32[512,128]{1,0:T(8,128)}, f32[1]{0:T(128)}) custom-call(s32[1,128]{1,0:T(1,128)S(1)} %get-tuple-element.15.starts_ref, f32[30592,128]{1,0:T(8,128)S(1)} %get-tuple-element.16.part_ref, f32[8,8,128]{2,1,0:T(8,128)S(1)} %get-tuple-element.17.st_ref, ...), custom_call_target="tpu_custom_call" | custom-call | tf_op jit(solution)/shard_map/finish/pallas_call | solution.py:528

commit v9 on v8

--- a/solution.py
+++ b/solution.py
@@ -17,7 +17,7 @@
 HEAD_BLOCK = 8192
 TABLE_BLOCK = 3648
 EMB_BLOCK = 2048
-WRITE_PARTS = 4
+WRITE_PARTS = 1
 TOKEN_VMEM = 46 * 1024 * 1024
 FINISH_VMEM = 28 * 1024 * 1024
 
@@ -151,10 +151,12 @@
             body(head_full * HEAD_BLOCK, vocab % HEAD_BLOCK)
 
     gat[...] = jnp.zeros_like(gat)
+    zero = jnp.minimum(joined_row(tok_ref, 0, tok_n), 0).astype(F32)
+    one = zero + 1.0
 
     def gather_block(v0, size):
         hot = jnp.concatenate(
-            [jnp.where(pick == lane2 + (v0 + j * tok_n), 1.0, 0.0).astype(BF16) for j in range(size // tok_n)], axis=1)
+            [jnp.where(pick == lane2 + (v0 + j * tok_n), one, zero).astype(BF16) for j in range(size // tok_n)], axis=1)
         gat[...] += dot_nn(hot, emb[pl.ds(v0, size), :])
 
     blocks(gather_block, 0, head_full // 2)
@@ -393,7 +395,7 @@
     for c in range(n_stage):
         acc = jnp.zeros((tok_n, dim), F32)
         for i in range(n_stage):
-            hot = jnp.where(rank_out[i:i + 1, :] == row_id + c * tok_n, 1.0, 0.0).astype(BF16)
+            hot = jnp.where(rank_out[i:i + 1, :] == row_id + c * tok_n, one, zero).astype(BF16)
             acc = acc + dot_nn(hot, dx_out[i])
         dxs[c] = acc.astype(BF16)
     dxs[n_stage] = jnp.zeros((tok_n, dim), BF16)
@@ -462,13 +464,16 @@
         copy.start()
     loss_ref[0] = jnp.sum(st_ref[:, 2, :]) * (1.0 / (n_chunk * tok_n))
 
+    mark = jnp.broadcast_to(ids_ref[n_chunk, 0:1, :].astype(F32), (16, tok_n))
+    one, zero = (-mark).astype(BF16)[0:1, :], (mark + 1.0).astype(BF16)[0:1, :]
+
     def add_tokens(j, size):
         rows = span(j, size)
         row16 = lax.broadcasted_iota(jnp.int16, (size, tok_n), 0)
 
         def hot_rows(c):
             ids = jnp.broadcast_to(ids_ref[c, 0:1, :] - j * EMB_BLOCK, (16, tok_n)).astype(jnp.int16)
-            return jnp.where(row16 == ids[0:1, :], jnp.ones((), BF16), jnp.zeros((), BF16))
+            return jnp.where(row16 == ids[0:1, :], one, zero)
 
         first = jnp.minimum(starts_sm[0, j] // tok_n, n_chunk - 1)
         last = (starts_sm[0, j + 1] + tok_n - 1) // tok_n

time: 64.8 us -> 64.4 us (level)
  no operation moved by 1% of the time
where the time goes in v9:
time: 64.4 us; the launch traced here: 64.3 us
  Pallas kernels  63.5 us (99%)
  between operations  0.82 us (1%)
    pallas_call x1, Pallas kernels, device_fn(): pl.pallas_call(functools.partial(token_kernel, n_stage), out_shape=[pltpu...  53.5 us
    pallas_call x1, Pallas kernels, device_fn(): pl.pallas_call(finish_kernel, out_shape=[jax.ShapeDtypeStruct((vocab, dim...  9.93 us

profile of v9, /device:TPU:81, one launch (start us, length us, event | category | flops | bytes accessed | tf_op | source)
XLA Modules:
  0.0 64.3 jit_solution(6184290990239993203)
XLA Ops:
  0.6 53.5 %token_pass.1 = (f32[8,8,128]{2,1,0:T(8,128)S(1)}, f32[30592,128]{1,0:T(8,128)S(1)}, s32[9,8,128]{2,1,0:T(8,128)S(1)}, s32[1,128]{1,0:T(1,128)S(1)}, bf16[9,128,...) custom-call(s32[16,64]{1,0:T(8,128)} %tok_hbm.1, s32[16,64]{1,0:T(8,128)} %lab_hbm.1, ...), custom_call_target="tpu_custom_call" | custom-call | tf_op jit(solution)/shard_map/token_pass/pallas_call | solution.py:510
  54.2 9.9 %finish.1 = (f32[30592,128]{1,0:T(8,128)}, f32[128,512]{1,0:T(8,128)}, f32[512,128]{1,0:T(8,128)}, f32[1]{0:T(128)}) custom-call(s32[1,128]{1,0:T(1,128)S(1)} %get-tuple-element.15.starts_ref, f32[30592,128]{1,0:T(8,128)S(1)} %get-tuple-element.16.part_ref, f32[8,8,128]{2,1,0:T(8,128)S(1)} %get-tuple-element.17.st_ref, ...), custom_call_target="tpu_custom_call" | custom-call | tf_op jit(solution)/shard_map/finish/pallas_call | solution.py:533

commit v10 on v9

--- a/solution.py
+++ b/solution.py
@@ -16,7 +16,7 @@
 GELU_C = math.sqrt(2.0 / math.pi)
 HEAD_BLOCK = 8192
 TABLE_BLOCK = 3648
-EMB_BLOCK = 2048
+EMB_BLOCK = 1024
 WRITE_PARTS = 1
 TOKEN_VMEM = 46 * 1024 * 1024
 FINISH_VMEM = 28 * 1024 * 1024

time: 64.4 us -> 66.5 us (1.033)
  Pallas kernels: 63.5 us -> 65.6 us
    pallas_call x1, Pallas kernels: 9.93 us -> 12.1 us  [device_fn(): pl.pallas_call(finish_kernel, out_shape=[jax.ShapeDtypeStruct((vocab, dim...]
where the time goes in v10:
time: 66.5 us; the launch traced here: 66.4 us
  Pallas kernels  65.6 us (99%)
  between operations  0.82 us (1%)
    pallas_call x1, Pallas kernels, device_fn(): pl.pallas_call(functools.partial(token_kernel, n_stage), out_shape=[pltpu...  53.5 us
    pallas_call x1, Pallas kernels, device_fn(): pl.pallas_call(finish_kernel, out_shape=[jax.ShapeDtypeStruct((vocab, dim...  12.1 us

profile of v10, /device:TPU:81, one launch (start us, length us, event | category | flops | bytes accessed | tf_op | source)
XLA Modules:
  0.0 66.4 jit_solution(7397500177755305144)
XLA Ops:
  0.6 53.5 %token_pass.1 = (f32[8,8,128]{2,1,0:T(8,128)S(1)}, f32[30592,128]{1,0:T(8,128)S(1)}, s32[9,8,128]{2,1,0:T(8,128)S(1)}, s32[1,128]{1,0:T(1,128)S(1)}, bf16[9,128,...) custom-call(s32[16,64]{1,0:T(8,128)} %tok_hbm.1, s32[16,64]{1,0:T(8,128)} %lab_hbm.1, ...), custom_call_target="tpu_custom_call" | custom-call | tf_op jit(solution)/shard_map/token_pass/pallas_call | solution.py:510
  54.2 12.1 %finish.1 = (f32[30592,128]{1,0:T(8,128)}, f32[128,512]{1,0:T(8,128)}, f32[512,128]{1,0:T(8,128)}, f32[1]{0:T(128)}) custom-call(s32[1,128]{1,0:T(1,128)S(1)} %get-tuple-element.15.starts_ref, f32[30592,128]{1,0:T(8,128)S(1)} %get-tuple-element.16.part_ref, f32[8,8,128]{2,1,0:T(8,128)S(1)} %get-tuple-element.17.st_ref, ...), custom_call_target="tpu_custom_call" | custom-call | tf_op jit(solution)/shard_map/finish/pallas_call | solution.py:533
